TPU v7x, 32 devices: a whole 2x2x4 slice. The times are simulated.
32 devices in a mesh: yy: 4 (over z), zz: 2 (over y), t: 4 (over x, core).
Axes of the slice: x: 2, y: 2, z: 4, core: 2. Of those that a mesh axis runs over, the one named last changes fastest.
Arguments:
- fat_links: float32 [4, 24, 12, 192, 20, 3, 3, 2], P(None, 't', 'zz', 'yy')
- long_links: float32 [4, 24, 12, 192, 20, 3, 3, 2], P(None, 't', 'zz', 'yy')
- source: float32 [24, 12, 192, 10, 3, 2], P('t', 'zz', 'yy')
- quark_mass: float32 [1], replicated
Outputs:
- output 1: float32 [24, 12, 192, 10, 3, 2], P('t', 'zz', 'yy')
- output 2: float32 [8], replicated
All inputs are finite; a program needn't handle non-finite values.
Results may differ from a plain program's by a relative error of at most 0.001.
Values are sent between devices in bfloat16 or wider.
A program may use at most 1 GiB of HBM per device.

v0:
```python
import jax
import jax.numpy as jnp
from jax import lax
from jax.sharding import PartitionSpec as P, NamedSharding

ITERS = 8
CUT_AXES = ('t', 'zz', 'yy')
ALL_AXES = ('yy', 'zz', 't')


def mat_vec(link_mat, colour_vec):
    link_re = link_mat[..., 0]
    link_im = link_mat[..., 1]
    vec_re = colour_vec[..., None, :, 0]
    vec_im = colour_vec[..., None, :, 1]
    return jnp.stack([jnp.sum(link_re * vec_re - link_im * vec_im, axis=-1), jnp.sum(link_re * vec_im + link_im * vec_re, axis=-1)], axis=-1)


def adj_vec(link_mat, colour_vec):
    link_re = link_mat[..., 0]
    link_im = link_mat[..., 1]
    vec_re = colour_vec[..., :, None, 0]
    vec_im = colour_vec[..., :, None, 1]
    return jnp.stack([jnp.sum(link_re * vec_re + link_im * vec_im, axis=-2), jnp.sum(link_re * vec_im - link_im * vec_re, axis=-2)], axis=-1)


def split_links(link_full, par_grid):
    n_dir, t_len, z_len, y_len, x_len = link_full.shape[:5]
    paired = link_full.reshape(n_dir, t_len, z_len, y_len, x_len // 2, 2, 3, 3, 2)
    par_links = par_grid[None, :, :, :, None, None, None, None]
    first_half = paired[:, :, :, :, :, 0]
    second_half = paired[:, :, :, :, :, 1]
    return jnp.where(par_links == 0, first_half, second_half), jnp.where(par_links == 0, second_half, first_half)


def value_a10(field_in, step_len, out_par, par_field):
    if out_par == 0:
        base_off = (step_len - 1) // 2
        odd_off = base_off + 1
    else:
        base_off = (step_len + 1) // 2
        odd_off = base_off - 1
    return jnp.where(par_field == 1, jnp.roll(field_in, -odd_off, axis=3), jnp.roll(field_in, -base_off, axis=3))


def cut_shifts(psi_in, chi_one, chi_three, axis_dim, n_dev):
    axis_name = CUT_AXES[axis_dim]
    length = psi_in.shape[axis_dim]
    to_prev = [(src_idx, (src_idx - 1) % n_dev) for src_idx in range(n_dev)]
    to_next = [(src_idx, (src_idx + 1) % n_dev) for src_idx in range(n_dev)]
    from_next = lax.ppermute(lax.slice_in_dim(psi_in, 0, 3, axis=axis_dim), axis_name, to_prev)
    back_send = jnp.concatenate([lax.slice_in_dim(chi_one, length - 1, length, axis=axis_dim), lax.slice_in_dim(chi_three, length - 3, length, axis=axis_dim)], axis=axis_dim)
    from_prev = lax.ppermute(back_send, axis_name, to_next)
    psi_ext = jnp.concatenate([psi_in, from_next], axis=axis_dim)
    plus_one = lax.slice_in_dim(psi_ext, 1, length + 1, axis=axis_dim)
    plus_three = lax.slice_in_dim(psi_ext, 3, length + 3, axis=axis_dim)
    minus_one = jnp.concatenate([lax.slice_in_dim(from_prev, 0, 1, axis=axis_dim), lax.slice_in_dim(chi_one, 0, length - 1, axis=axis_dim)], axis=axis_dim)
    minus_three = jnp.concatenate([lax.slice_in_dim(from_prev, 1, 4, axis=axis_dim), lax.slice_in_dim(chi_three, 0, length - 3, axis=axis_dim)], axis=axis_dim)
    return plus_one, plus_three, minus_one, minus_three


def local_hop(psi_in, out_par, fat_out, fat_in, long_out, long_in, par_field, cut_sizes):
    total = jnp.zeros_like(psi_in)
    for direction in range(3):
        chi_one = adj_vec(fat_in[direction], psi_in)
        chi_three = adj_vec(long_in[direction], psi_in)
        plus_one, plus_three, minus_one, minus_three = cut_shifts(psi_in, chi_one, chi_three, direction, cut_sizes[direction])
        total = total + mat_vec(fat_out[direction], plus_one) + mat_vec(long_out[direction], plus_three) - minus_one - minus_three
    chi_one = adj_vec(fat_in[3], psi_in)
    chi_three = adj_vec(long_in[3], psi_in)
    total = total + mat_vec(fat_out[3], value_a10(psi_in, 1, out_par, par_field)) + mat_vec(long_out[3], value_a10(psi_in, 3, out_par, par_field)) - value_a10(chi_one, -1, out_par, par_field) - value_a10(chi_three, -3, out_par, par_field)
    return total


def solution(mesh):
    cut_sizes = tuple(mesh.shape[axis_label] for axis_label in CUT_AXES)
    link_spec = P(None, 't', 'zz', 'yy', None, None, None, None)
    field_spec = P('t', 'zz', 'yy', None, None, None)

    def local_solve(fat_links, long_links, source, quark_mass):
        t_len, z_len, y_len = source.shape[:3]
        t_coord = lax.axis_index('t') * t_len + jnp.arange(t_len)
        z_coord = lax.axis_index('zz') * z_len + jnp.arange(z_len)
        y_coord = lax.axis_index('yy') * y_len + jnp.arange(y_len)
        par_grid = (t_coord[:, None, None] + z_coord[None, :, None] + y_coord[None, None, :]) % 2
        par_field = par_grid[:, :, :, None, None, None]
        fat_even, fat_odd = split_links(fat_links, par_grid)
        long_even, long_odd = split_links(long_links, par_grid)
        mass_sq = quark_mass[0] * quark_mass[0]
        src_norm = lax.psum(jnp.sum(source * source), ALL_AXES)
        sol_vec = jnp.zeros_like(source)
        res_vec = source
        search_dir = source
        res_norm = src_norm
        history = []
        for step_idx in range(ITERS):
            odd_part = local_hop(search_dir, 1, fat_odd, fat_even, long_odd, long_even, par_field, cut_sizes)
            applied = mass_sq * search_dir - local_hop(odd_part, 0, fat_even, fat_odd, long_even, long_odd, par_field, cut_sizes)
            step_size = res_norm / lax.psum(jnp.sum(search_dir * applied), ALL_AXES)
            sol_vec = sol_vec + step_size * search_dir
            res_vec = res_vec - step_size * applied
            new_norm = lax.psum(jnp.sum(res_vec * res_vec), ALL_AXES)
            history.append(new_norm / src_norm)
            search_dir = res_vec + (new_norm / res_norm) * search_dir
            res_norm = new_norm
        return sol_vec, jnp.stack(history)

    return jax.shard_map(local_solve, mesh=mesh, in_specs=(link_spec, link_spec, field_spec, P(None)), out_specs=(field_spec, P()), check_vma=False)
```

profile of v0, /device:TPU:0, one launch (start us, length us, event | category | flops | bytes accessed | tf_op | source)
XLA Modules:
  0.0 3608.8 jit_solution(15823295345431558493)
XLA Ops:
  15.5 35.5 fusion.880
  51.0 53.3 %fusion.1 = (f32[4,6,6,48,10,3,3,2]{3,6,5,4,2,1,7,0:T(4,128)}, f32[4,6,6,48,10,3,3,2]{3,6,5,4,2,1,7,0:T(4,128)}, f32[4,6,6,48,10,3,3,2]{3,6,5,4,2,1,7,0:T(4,128)}, f32[4,6,6,48,10,3,3,2]{3,6,5,4,2,1,7,0:T(4,128)}) fusion(f32[4,6,6,48,10,1,3,3,2]{3,8,7,6,5,4,2,1,0:T(2,128)} %get-tuple-element.745, f32[4,6,6,48,10,1,3,3,2]{3,8,7,6,5,4,2,1,0:T(2,128)} %get-tuple-element.744, ...), kind=kLoop, calls=%fused_computation.2 | loop fusion | flops 4976640 | bytes 39814848 | tf_op jit(solution)/shard_map/jit(_where)/select_n | solution.py:33
  104.3 12.9 slice_bitcast_fusion.8
  117.2 12.9 slice_bitcast_fusion.9
  130.0 12.3 slice_bitcast_fusion.2
  142.4 13.6 slice_bitcast_fusion.3
  191.0 25.7 add_reduce_fusion.253
  351.9 26.4 add_reduce_fusion.237
  469.1 10.5 multiply_reduce_fusion.15
  479.7 39.1 %all-reduce = (f32[]{:T(128)}, f32[]{:T(128)}) all-reduce(f32[]{:T(128)} %multiply_reduce_fusion.16, f32[]{:T(128)} %get-tuple-element.738), channel_id=1, replica_groups=mesh['yy'=4,'zz'=2,'t'=4] {'yy','zz','t'}, use_global_device_ids=true, to_apply=%region_1.2 | all-reduce | flops 2 | bytes 16 | tf_op jit(solution)/shard_map/psum | solution.py:90
  521.1 41.7 %psum.121 = f32[]{:T(128)} all-reduce(f32[]{:T(128)} %multiply_reduce_fusion.14), channel_id=1, replica_groups=mesh['yy'=4,'zz'=2,'t'=4] {'yy','zz','t'}, use_global_device_ids=true, to_apply=%region_69.70 | all-reduce | flops 1 | bytes 8 | tf_op jit(solution)/shard_map/psum | solution.py:102
  609.3 25.6 add_reduce_fusion.221
  718.1 9.6 fusion.52
  774.9 26.1 add_reduce_fusion.205
  895.8 11.6 multiply_reduce_fusion.13
  907.4 40.0 %psum.122 = f32[]{:T(128)} all-reduce(f32[]{:T(128)} %get-tuple-element.736), channel_id=1, replica_groups=mesh['yy'=4,'zz'=2,'t'=4] {'yy','zz','t'}, use_global_device_ids=true, to_apply=%region_135.136 | all-reduce | flops 1 | bytes 8 | tf_op jit(solution)/shard_map/psum | solution.py:99
  952.6 41.5 %psum.123 = f32[]{:T(128)} all-reduce(f32[]{:T(128)} %get-tuple-element.734), channel_id=1, replica_groups=mesh['yy'=4,'zz'=2,'t'=4] {'yy','zz','t'}, use_global_device_ids=true, to_apply=%region_137.138 | all-reduce | flops 1 | bytes 8 | tf_op jit(solution)/shard_map/psum | solution.py:102
  1044.2 25.9 add_reduce_fusion.189
  1210.0 26.3 add_reduce_fusion.173
  1330.4 11.7 multiply_reduce_fusion.11
  1342.1 39.4 %psum.124 = f32[]{:T(128)} all-reduce(f32[]{:T(128)} %get-tuple-element.732), channel_id=1, replica_groups=mesh['yy'=4,'zz'=2,'t'=4] {'yy','zz','t'}, use_global_device_ids=true, to_apply=%region_203.204 | all-reduce | flops 1 | bytes 8 | tf_op jit(solution)/shard_map/psum | solution.py:99
  1386.3 41.7 %psum.125 = f32[]{:T(128)} all-reduce(f32[]{:T(128)} %get-tuple-element.730), channel_id=1, replica_groups=mesh['yy'=4,'zz'=2,'t'=4] {'yy','zz','t'}, use_global_device_ids=true, to_apply=%region_205.206 | all-reduce | flops 1 | bytes 8 | tf_op jit(solution)/shard_map/psum | solution.py:102
  1478.0 25.7 add_reduce_fusion.157
  1643.7 26.3 add_reduce_fusion.141
  1764.4 11.8 multiply_reduce_fusion.9
  1776.2 39.5 %psum.126 = f32[]{:T(128)} all-reduce(f32[]{:T(128)} %get-tuple-element.728), channel_id=1, replica_groups=mesh['yy'=4,'zz'=2,'t'=4] {'yy','zz','t'}, use_global_device_ids=true, to_apply=%region_271.272 | all-reduce | flops 1 | bytes 8 | tf_op jit(solution)/shard_map/psum | solution.py:99
  1820.5 41.5 %psum.127 = f32[]{:T(128)} all-reduce(f32[]{:T(128)} %get-tuple-element.726), channel_id=1, replica_groups=mesh['yy'=4,'zz'=2,'t'=4] {'yy','zz','t'}, use_global_device_ids=true, to_apply=%region_273.274 | all-reduce | flops 1 | bytes 8 | tf_op jit(solution)/shard_map/psum | solution.py:102
  1912.1 25.9 add_reduce_fusion.125
  2021.3 9.6 fusion.31
  2077.8 26.4 add_reduce_fusion.109
  2198.5 11.7 multiply_reduce_fusion.7
  2210.1 39.4 %psum.128 = f32[]{:T(128)} all-reduce(f32[]{:T(128)} %get-tuple-element.724), channel_id=1, replica_groups=mesh['yy'=4,'zz'=2,'t'=4] {'yy','zz','t'}, use_global_device_ids=true, to_apply=%region_339.340 | all-reduce | flops 1 | bytes 8 | tf_op jit(solution)/shard_map/psum | solution.py:99
  2254.3 41.7 %psum.129 = f32[]{:T(128)} all-reduce(f32[]{:T(128)} %get-tuple-element.722), channel_id=1, replica_groups=mesh['yy'=4,'zz'=2,'t'=4] {'yy','zz','t'}, use_global_device_ids=true, to_apply=%region_341.342 | all-reduce | flops 1 | bytes 8 | tf_op jit(solution)/shard_map/psum | solution.py:102
  2345.9 25.7 add_reduce_fusion.93
  2511.7 26.2 add_reduce_fusion.77
  2632.2 11.7 multiply_reduce_fusion.5
  2643.9 39.4 %psum.130 = f32[]{:T(128)} all-reduce(f32[]{:T(128)} %get-tuple-element.720), channel_id=1, replica_groups=mesh['yy'=4,'zz'=2,'t'=4] {'yy','zz','t'}, use_global_device_ids=true, to_apply=%region_407.408 | all-reduce | flops 1 | bytes 8 | tf_op jit(solution)/shard_map/psum | solution.py:99
  2688.1 41.5 %psum.131 = f32[]{:T(128)} all-reduce(f32[]{:T(128)} %get-tuple-element.718), channel_id=1, replica_groups=mesh['yy'=4,'zz'=2,'t'=4] {'yy','zz','t'}, use_global_device_ids=true, to_apply=%region_409.410 | all-reduce | flops 1 | bytes 8 | tf_op jit(solution)/shard_map/psum | solution.py:102
  2779.8 25.9 add_reduce_fusion.61
  2945.5 26.4 add_reduce_fusion.45
  3066.0 11.7 multiply_reduce_fusion.3
  3077.7 39.4 %psum.132 = f32[]{:T(128)} all-reduce(f32[]{:T(128)} %get-tuple-element.716), channel_id=1, replica_groups=mesh['yy'=4,'zz'=2,'t'=4] {'yy','zz','t'}, use_global_device_ids=true, to_apply=%region_475.476 | all-reduce | flops 1 | bytes 8 | tf_op jit(solution)/shard_map/psum | solution.py:99
  3121.9 41.7 %psum.133 = f32[]{:T(128)} all-reduce(f32[]{:T(128)} %get-tuple-element.714), channel_id=1, replica_groups=mesh['yy'=4,'zz'=2,'t'=4] {'yy','zz','t'}, use_global_device_ids=true, to_apply=%region_477.478 | all-reduce | flops 1 | bytes 8 | tf_op jit(solution)/shard_map/psum | solution.py:102
  3213.8 25.7 add_reduce_fusion.29
  3379.8 26.1 add_reduce_fusion.13
  3501.9 11.3 multiply_reduce_fusion.1
  3513.2 39.6 %psum.134 = f32[]{:T(128)} all-reduce(f32[]{:T(128)} %get-tuple-element.712), channel_id=1, replica_groups=mesh['yy'=4,'zz'=2,'t'=4] {'yy','zz','t'}, use_global_device_ids=true, to_apply=%region_543.544 | all-reduce | flops 1 | bytes 8 | tf_op jit(solution)/shard_map/psum | solution.py:99
  3562.4 41.3 %psum.135 = f32[]{:T(128)} all-reduce(f32[]{:T(128)} %multiply_reduce_fusion), channel_id=1, replica_groups=mesh['yy'=4,'zz'=2,'t'=4] {'yy','zz','t'}, use_global_device_ids=true, to_apply=%region_545.546 | all-reduce | flops 1 | bytes 8 | tf_op jit(solution)/shard_map/psum | solution.py:102
  (4013 shorter events, 2242.4 us)
Async XLA Ops:
  3.9 170.6 %collective-permute-start.4 = (f32[6,6,3,10,3,2]{3,5,4,2,1,0:T(2,128)}, f32[6,6,3,10,3,2]{3,5,4,2,1,0:T(2,128)}, u32[]{:S(2)}, u32[]{:S(2)}) collective-permute-start(f32[6,6,3,10,3,2]{3,5,4,2,1,0:T(2,128)} %copy.1365), channel_id=1, source_target_pairs={{0,24},{8,0},{16,8},{24,16},{1,25},{9,1},{17,9},{25,17},{2,26},{10... | collective-permute-start | bytes 77768 | tf_op jit(solution)/shard_map/ppermute | solution.py:51
  11.1 167.4 %collective-permute-start.2 = (f32[6,3,48,10,3,2]{2,5,4,3,1,0:T(2,128)}, f32[6,3,48,10,3,2]{2,5,4,3,1,0:T(2,128)}, u32[]{:S(2)}, u32[]{:S(2)}) collective-permute-start(f32[6,3,48,10,3,2]{2,5,4,3,1,0:T(2,128)} %slice.3811), channel_id=1, source_target_pairs={{0,4},{4,0},{1,5},{5,1},{2,6},{6,2},{3,7},{7,3},{8,12},{12,8},{9,1... | collective-permute-start | bytes 622088 | tf_op jit(solution)/shard_map/ppermute | solution.py:51
  13.6 224.9 %collective-permute-start = (f32[3,6,48,10,3,2]{2,5,4,3,1,0:T(2,128)}, f32[3,6,48,10,3,2]{2,5,4,3,1,0:T(2,128)}, u32[]{:S(2)}, u32[]{:S(2)}) collective-permute-start(f32[3,6,48,10,3,2]{2,5,4,3,1,0:T(2,128)} %slice.3786), channel_id=1, source_target_pairs={{0,3},{1,0},{2,1},{3,2},{4,7},{5,4},{6,5},{7,6},{8,11},{9,8},{10,9... | collective-permute-start | bytes 622088 | tf_op jit(solution)/shard_map/ppermute | solution.py:51
  228.0 58.1 %collective-permute-start.5 = (f32[6,6,4,10,3,2]{3,2,5,4,1,0:T(4,128)S(1)}, f32[6,6,4,10,3,2]{3,2,5,4,1,0:T(4,128)S(1)}, u32[]{:S(2)}, u32[]{:S(2)}) collective-permute-start(f32[6,6,4,10,3,2]{3,2,5,4,1,0:T(4,128)S(1)} %pad_maximum_fusion.239), channel_id=1, source_target_pairs={{0,8},{8,16},{16,24},{24,0},{1,9},{9,17},{17,25},{25,1},{2,10},{10... | collective-permute-start | bytes 103688 | tf_op jit(solution)/shard_map/ppermute | solution.py:53
  232.0 61.5 %collective-permute-start.3 = (f32[6,4,48,10,3,2]{2,1,5,4,3,0:T(4,128)}, f32[6,4,48,10,3,2]{2,1,5,4,3,0:T(4,128)S(1)}, u32[]{:S(2)}, u32[]{:S(2)}) collective-permute-start(f32[6,4,48,10,3,2]{2,1,5,4,3,0:T(4,128)} %fusion.835), channel_id=1, source_target_pairs={{0,4},{4,0},{1,5},{5,1},{2,6},{6,2},{3,7},{7,3},{8,12},{12,8},{9,1... | collective-permute-start | bytes 829448 | tf_op jit(solution)/shard_map/ppermute | solution.py:53
  319.4 64.4 %collective-permute-start.8 = (f32[6,3,48,10,3,2]{2,5,4,3,1,0:T(2,128)}, f32[6,3,48,10,3,2]{2,5,4,3,1,0:T(2,128)}, u32[]{:S(2)}, u32[]{:S(2)}) collective-permute-start(f32[6,3,48,10,3,2]{2,5,4,3,1,0:T(2,128)} %copy.428), channel_id=1, source_target_pairs={{0,4},{4,0},{1,5},{5,1},{2,6},{6,2},{3,7},{7,3},{8,12},{12,8},{9,1... | collective-permute-start | bytes 622088 | tf_op jit(solution)/shard_map/ppermute | solution.py:51
  383.9 79.5 %collective-permute-start.7 = (f32[4,6,48,10,3,2]{2,0,5,4,3,1:T(4,128)}, f32[4,6,48,10,3,2]{2,0,5,4,3,1:T(4,128)}, u32[]{:S(2)}, u32[]{:S(2)}) collective-permute-start(f32[4,6,48,10,3,2]{2,0,5,4,3,1:T(4,128)} %copy.425), channel_id=1, source_target_pairs={{0,1},{1,2},{2,3},{3,0},{4,5},{5,6},{6,7},{7,4},{8,9},{9,10},{10,1... | collective-permute-start | bytes 829448 | tf_op jit(solution)/shard_map/ppermute | solution.py:53
  392.9 73.6 %collective-permute-start.9 = (f32[6,4,48,10,3,2]{2,1,5,4,3,0:T(4,128)}, f32[6,4,48,10,3,2]{2,1,5,4,3,0:T(4,128)}, u32[]{:S(2)}, u32[]{:S(2)}) collective-permute-start(f32[6,4,48,10,3,2]{2,1,5,4,3,0:T(4,128)} %fusion.831), channel_id=1, source_target_pairs={{0,4},{4,0},{1,5},{5,1},{2,6},{6,2},{3,7},{7,3},{8,12},{12,8},{9,1... | collective-permute-start | bytes 829448 | tf_op jit(solution)/shard_map/ppermute | solution.py:53
  593.4 69.1 %collective-permute-start.12 = (f32[3,6,48,10,3,2]{2,5,4,3,1,0:T(2,128)}, f32[3,6,48,10,3,2]{2,5,4,3,1,0:T(2,128)}, u32[]{:S(2)}, u32[]{:S(2)}) collective-permute-start(f32[3,6,48,10,3,2]{2,5,4,3,1,0:T(2,128)} %copy.476), channel_id=1, source_target_pairs={{0,3},{1,0},{2,1},{3,2},{4,7},{5,4},{6,5},{7,6},{8,11},{9,8},{10,9... | collective-permute-start | bytes 622088 | tf_op jit(solution)/shard_map/ppermute | solution.py:51
  654.8 60.6 %collective-permute-start.15 = (f32[6,4,48,10,3,2]{2,1,5,4,3,0:T(4,128)}, f32[6,4,48,10,3,2]{2,1,5,4,3,0:T(4,128)}, u32[]{:S(2)}, u32[]{:S(2)}) collective-permute-start(f32[6,4,48,10,3,2]{2,1,5,4,3,0:T(4,128)} %fusion.827), channel_id=1, source_target_pairs={{0,4},{4,0},{1,5},{5,1},{2,6},{6,2},{3,7},{7,3},{8,12},{12,8},{9,1... | collective-permute-start | bytes 829448 | tf_op jit(solution)/shard_map/ppermute | solution.py:53
  742.0 64.6 %collective-permute-start.20 = (f32[6,3,48,10,3,2]{2,5,4,3,1,0:T(2,128)}, f32[6,3,48,10,3,2]{2,5,4,3,1,0:T(2,128)}, u32[]{:S(2)}, u32[]{:S(2)}) collective-permute-start(f32[6,3,48,10,3,2]{2,5,4,3,1,0:T(2,128)} %copy.558), channel_id=1, source_target_pairs={{0,4},{4,0},{1,5},{5,1},{2,6},{6,2},{3,7},{7,3},{8,12},{12,8},{9,1... | collective-permute-start | bytes 622088 | tf_op jit(solution)/shard_map/ppermute | solution.py:51
  806.6 83.4 %collective-permute-start.19 = (f32[4,6,48,10,3,2]{2,0,5,4,3,1:T(4,128)}, f32[4,6,48,10,3,2]{2,0,5,4,3,1:T(4,128)}, u32[]{:S(2)}, u32[]{:S(2)}) collective-permute-start(f32[4,6,48,10,3,2]{2,0,5,4,3,1:T(4,128)} %copy.555), channel_id=1, source_target_pairs={{0,1},{1,2},{2,3},{3,0},{4,5},{5,6},{6,7},{7,4},{8,9},{9,10},{10,1... | collective-permute-start | bytes 829448 | tf_op jit(solution)/shard_map/ppermute | solution.py:53
  815.5 77.6 %collective-permute-start.21 = (f32[6,4,48,10,3,2]{2,1,5,4,3,0:T(4,128)}, f32[6,4,48,10,3,2]{2,1,5,4,3,0:T(4,128)}, u32[]{:S(2)}, u32[]{:S(2)}) collective-permute-start(f32[6,4,48,10,3,2]{2,1,5,4,3,0:T(4,128)} %fusion.823), channel_id=1, source_target_pairs={{0,4},{4,0},{1,5},{5,1},{2,6},{6,2},{3,7},{7,3},{8,12},{12,8},{9,1... | collective-permute-start | bytes 829448 | tf_op jit(solution)/shard_map/ppermute | solution.py:53
  1028.4 69.1 %collective-permute-start.24 = (f32[3,6,48,10,3,2]{2,5,4,3,1,0:T(2,128)}, f32[3,6,48,10,3,2]{2,5,4,3,1,0:T(2,128)}, u32[]{:S(2)}, u32[]{:S(2)}) collective-permute-start(f32[3,6,48,10,3,2]{2,5,4,3,1,0:T(2,128)} %copy.602), channel_id=1, source_target_pairs={{0,3},{1,0},{2,1},{3,2},{4,7},{5,4},{6,5},{7,6},{8,11},{9,8},{10,9... | collective-permute-start | bytes 622088 | tf_op jit(solution)/shard_map/ppermute | solution.py:51
  1083.9 56.8 %collective-permute-start.29 = (f32[6,6,4,10,3,2]{3,2,5,4,1,0:T(4,128)S(1)}, f32[6,6,4,10,3,2]{3,2,5,4,1,0:T(4,128)S(1)}, u32[]{:S(2)}, u32[]{:S(2)}) collective-permute-start(f32[6,6,4,10,3,2]{3,2,5,4,1,0:T(4,128)S(1)} %pad_maximum_fusion.243), channel_id=1, source_target_pairs={{0,8},{8,16},{16,24},{24,0},{1,9},{9,17},{17,25},{25,1},{2,10},{10... | collective-permute-start | bytes 103688 | tf_op jit(solution)/shard_map/ppermute | solution.py:53
  1089.8 60.8 %collective-permute-start.27 = (f32[6,4,48,10,3,2]{2,1,5,4,3,0:T(4,128)}, f32[6,4,48,10,3,2]{2,1,5,4,3,0:T(4,128)}, u32[]{:S(2)}, u32[]{:S(2)}) collective-permute-start(f32[6,4,48,10,3,2]{2,1,5,4,3,0:T(4,128)} %fusion.819), channel_id=1, source_target_pairs={{0,4},{4,0},{1,5},{5,1},{2,6},{6,2},{3,7},{7,3},{8,12},{12,8},{9,1... | collective-permute-start | bytes 829448 | tf_op jit(solution)/shard_map/ppermute | solution.py:53
  1176.9 65.0 %collective-permute-start.32 = (f32[6,3,48,10,3,2]{2,5,4,3,1,0:T(2,128)}, f32[6,3,48,10,3,2]{2,5,4,3,1,0:T(2,128)}, u32[]{:S(2)}, u32[]{:S(2)}) collective-permute-start(f32[6,3,48,10,3,2]{2,5,4,3,1,0:T(2,128)} %copy.684), channel_id=1, source_target_pairs={{0,4},{4,0},{1,5},{5,1},{2,6},{6,2},{3,7},{7,3},{8,12},{12,8},{9,1... | collective-permute-start | bytes 622088 | tf_op jit(solution)/shard_map/ppermute | solution.py:51
  1241.9 82.7 %collective-permute-start.31 = (f32[4,6,48,10,3,2]{2,0,5,4,3,1:T(4,128)}, f32[4,6,48,10,3,2]{2,0,5,4,3,1:T(4,128)}, u32[]{:S(2)}, u32[]{:S(2)}) collective-permute-start(f32[4,6,48,10,3,2]{2,0,5,4,3,1:T(4,128)} %copy.681), channel_id=1, source_target_pairs={{0,1},{1,2},{2,3},{3,0},{4,5},{5,6},{6,7},{7,4},{8,9},{9,10},{10,1... | collective-permute-start | bytes 829448 | tf_op jit(solution)/shard_map/ppermute | solution.py:53
  1250.8 76.9 %collective-permute-start.33 = (f32[6,4,48,10,3,2]{2,1,5,4,3,0:T(4,128)}, f32[6,4,48,10,3,2]{2,1,5,4,3,0:T(4,128)}, u32[]{:S(2)}, u32[]{:S(2)}) collective-permute-start(f32[6,4,48,10,3,2]{2,1,5,4,3,0:T(4,128)} %fusion.815), channel_id=1, source_target_pairs={{0,4},{4,0},{1,5},{5,1},{2,6},{6,2},{3,7},{7,3},{8,12},{12,8},{9,1... | collective-permute-start | bytes 829448 | tf_op jit(solution)/shard_map/ppermute | solution.py:53
  1462.2 68.9 %collective-permute-start.36 = (f32[3,6,48,10,3,2]{2,5,4,3,1,0:T(2,128)}, f32[3,6,48,10,3,2]{2,5,4,3,1,0:T(2,128)}, u32[]{:S(2)}, u32[]{:S(2)}) collective-permute-start(f32[3,6,48,10,3,2]{2,5,4,3,1,0:T(2,128)} %copy.728), channel_id=1, source_target_pairs={{0,3},{1,0},{2,1},{3,2},{4,7},{5,4},{6,5},{7,6},{8,11},{9,8},{10,9... | collective-permute-start | bytes 622088 | tf_op jit(solution)/shard_map/ppermute | solution.py:51
  1517.5 56.9 %collective-permute-start.41 = (f32[6,6,4,10,3,2]{3,2,5,4,1,0:T(4,128)S(1)}, f32[6,6,4,10,3,2]{3,2,5,4,1,0:T(4,128)S(1)}, u32[]{:S(2)}, u32[]{:S(2)}) collective-permute-start(f32[6,6,4,10,3,2]{3,2,5,4,1,0:T(4,128)S(1)} %pad_maximum_fusion.245), channel_id=1, source_target_pairs={{0,8},{8,16},{16,24},{24,0},{1,9},{9,17},{17,25},{25,1},{2,10},{10... | collective-permute-start | bytes 103688 | tf_op jit(solution)/shard_map/ppermute | solution.py:53
  1523.5 60.8 %collective-permute-start.39 = (f32[6,4,48,10,3,2]{2,1,5,4,3,0:T(4,128)}, f32[6,4,48,10,3,2]{2,1,5,4,3,0:T(4,128)}, u32[]{:S(2)}, u32[]{:S(2)}) collective-permute-start(f32[6,4,48,10,3,2]{2,1,5,4,3,0:T(4,128)} %fusion.811), channel_id=1, source_target_pairs={{0,4},{4,0},{1,5},{5,1},{2,6},{6,2},{3,7},{7,3},{8,12},{12,8},{9,1... | collective-permute-start | bytes 829448 | tf_op jit(solution)/shard_map/ppermute | solution.py:53
  1610.9 64.7 %collective-permute-start.44 = (f32[6,3,48,10,3,2]{2,5,4,3,1,0:T(2,128)}, f32[6,3,48,10,3,2]{2,5,4,3,1,0:T(2,128)}, u32[]{:S(2)}, u32[]{:S(2)}) collective-permute-start(f32[6,3,48,10,3,2]{2,5,4,3,1,0:T(2,128)} %copy.810), channel_id=1, source_target_pairs={{0,4},{4,0},{1,5},{5,1},{2,6},{6,2},{3,7},{7,3},{8,12},{12,8},{9,1... | collective-permute-start | bytes 622088 | tf_op jit(solution)/shard_map/ppermute | solution.py:51
  1675.6 83.1 %collective-permute-start.43 = (f32[4,6,48,10,3,2]{2,0,5,4,3,1:T(4,128)}, f32[4,6,48,10,3,2]{2,0,5,4,3,1:T(4,128)}, u32[]{:S(2)}, u32[]{:S(2)}) collective-permute-start(f32[4,6,48,10,3,2]{2,0,5,4,3,1:T(4,128)} %copy.807), channel_id=1, source_target_pairs={{0,1},{1,2},{2,3},{3,0},{4,5},{5,6},{6,7},{7,4},{8,9},{9,10},{10,1... | collective-permute-start | bytes 829448 | tf_op jit(solution)/shard_map/ppermute | solution.py:53
  1684.6 77.2 %collective-permute-start.45 = (f32[6,4,48,10,3,2]{2,1,5,4,3,0:T(4,128)}, f32[6,4,48,10,3,2]{2,1,5,4,3,0:T(4,128)}, u32[]{:S(2)}, u32[]{:S(2)}) collective-permute-start(f32[6,4,48,10,3,2]{2,1,5,4,3,0:T(4,128)} %fusion.807), channel_id=1, source_target_pairs={{0,4},{4,0},{1,5},{5,1},{2,6},{6,2},{3,7},{7,3},{8,12},{12,8},{9,1... | collective-permute-start | bytes 829448 | tf_op jit(solution)/shard_map/ppermute | solution.py:53
  1896.1 69.4 %collective-permute-start.48 = (f32[3,6,48,10,3,2]{2,5,4,3,1,0:T(2,128)}, f32[3,6,48,10,3,2]{2,5,4,3,1,0:T(2,128)}, u32[]{:S(2)}, u32[]{:S(2)}) collective-permute-start(f32[3,6,48,10,3,2]{2,5,4,3,1,0:T(2,128)} %copy.854), channel_id=1, source_target_pairs={{0,3},{1,0},{2,1},{3,2},{4,7},{5,4},{6,5},{7,6},{8,11},{9,8},{10,9... | collective-permute-start | bytes 622088 | tf_op jit(solution)/shard_map/ppermute | solution.py:51
  1957.8 60.8 %collective-permute-start.51 = (f32[6,4,48,10,3,2]{2,1,5,4,3,0:T(4,128)}, f32[6,4,48,10,3,2]{2,1,5,4,3,0:T(4,128)}, u32[]{:S(2)}, u32[]{:S(2)}) collective-permute-start(f32[6,4,48,10,3,2]{2,1,5,4,3,0:T(4,128)} %fusion.803), channel_id=1, source_target_pairs={{0,4},{4,0},{1,5},{5,1},{2,6},{6,2},{3,7},{7,3},{8,12},{12,8},{9,1... | collective-permute-start | bytes 829448 | tf_op jit(solution)/shard_map/ppermute | solution.py:53
  2044.9 65.0 %collective-permute-start.56 = (f32[6,3,48,10,3,2]{2,5,4,3,1,0:T(2,128)}, f32[6,3,48,10,3,2]{2,5,4,3,1,0:T(2,128)}, u32[]{:S(2)}, u32[]{:S(2)}) collective-permute-start(f32[6,3,48,10,3,2]{2,5,4,3,1,0:T(2,128)} %copy.936), channel_id=1, source_target_pairs={{0,4},{4,0},{1,5},{5,1},{2,6},{6,2},{3,7},{7,3},{8,12},{12,8},{9,1... | collective-permute-start | bytes 622088 | tf_op jit(solution)/shard_map/ppermute | solution.py:51
  2109.9 82.8 %collective-permute-start.55 = (f32[4,6,48,10,3,2]{2,0,5,4,3,1:T(4,128)}, f32[4,6,48,10,3,2]{2,0,5,4,3,1:T(4,128)}, u32[]{:S(2)}, u32[]{:S(2)}) collective-permute-start(f32[4,6,48,10,3,2]{2,0,5,4,3,1:T(4,128)} %copy.933), channel_id=1, source_target_pairs={{0,1},{1,2},{2,3},{3,0},{4,5},{5,6},{6,7},{7,4},{8,9},{9,10},{10,1... | collective-permute-start | bytes 829448 | tf_op jit(solution)/shard_map/ppermute | solution.py:53
  2118.8 77.0 %collective-permute-start.57 = (f32[6,4,48,10,3,2]{2,1,5,4,3,0:T(4,128)}, f32[6,4,48,10,3,2]{2,1,5,4,3,0:T(4,128)}, u32[]{:S(2)}, u32[]{:S(2)}) collective-permute-start(f32[6,4,48,10,3,2]{2,1,5,4,3,0:T(4,128)} %fusion.799), channel_id=1, source_target_pairs={{0,4},{4,0},{1,5},{5,1},{2,6},{6,2},{3,7},{7,3},{8,12},{12,8},{9,1... | collective-permute-start | bytes 829448 | tf_op jit(solution)/shard_map/ppermute | solution.py:53
  2330.1 69.0 %collective-permute-start.60 = (f32[3,6,48,10,3,2]{2,5,4,3,1,0:T(2,128)}, f32[3,6,48,10,3,2]{2,5,4,3,1,0:T(2,128)}, u32[]{:S(2)}, u32[]{:S(2)}) collective-permute-start(f32[3,6,48,10,3,2]{2,5,4,3,1,0:T(2,128)} %copy.980), channel_id=1, source_target_pairs={{0,3},{1,0},{2,1},{3,2},{4,7},{5,4},{6,5},{7,6},{8,11},{9,8},{10,9... | collective-permute-start | bytes 622088 | tf_op jit(solution)/shard_map/ppermute | solution.py:51
  2385.4 56.8 %collective-permute-start.65 = (f32[6,6,4,10,3,2]{3,2,5,4,1,0:T(4,128)S(1)}, f32[6,6,4,10,3,2]{3,2,5,4,1,0:T(4,128)S(1)}, u32[]{:S(2)}, u32[]{:S(2)}) collective-permute-start(f32[6,6,4,10,3,2]{3,2,5,4,1,0:T(4,128)S(1)} %pad_maximum_fusion.249), channel_id=1, source_target_pairs={{0,8},{8,16},{16,24},{24,0},{1,9},{9,17},{17,25},{25,1},{2,10},{10... | collective-permute-start | bytes 103688 | tf_op jit(solution)/shard_map/ppermute | solution.py:53
  2391.5 60.7 %collective-permute-start.63 = (f32[6,4,48,10,3,2]{2,1,5,4,3,0:T(4,128)}, f32[6,4,48,10,3,2]{2,1,5,4,3,0:T(4,128)}, u32[]{:S(2)}, u32[]{:S(2)}) collective-permute-start(f32[6,4,48,10,3,2]{2,1,5,4,3,0:T(4,128)} %fusion.795), channel_id=1, source_target_pairs={{0,4},{4,0},{1,5},{5,1},{2,6},{6,2},{3,7},{7,3},{8,12},{12,8},{9,1... | collective-permute-start | bytes 829448 | tf_op jit(solution)/shard_map/ppermute | solution.py:53
  2478.7 64.8 %collective-permute-start.68 = (f32[6,3,48,10,3,2]{2,5,4,3,1,0:T(2,128)}, f32[6,3,48,10,3,2]{2,5,4,3,1,0:T(2,128)}, u32[]{:S(2)}, u32[]{:S(2)}) collective-permute-start(f32[6,3,48,10,3,2]{2,5,4,3,1,0:T(2,128)} %copy.1062), channel_id=1, source_target_pairs={{0,4},{4,0},{1,5},{5,1},{2,6},{6,2},{3,7},{7,3},{8,12},{12,8},{9,1... | collective-permute-start | bytes 622088 | tf_op jit(solution)/shard_map/ppermute | solution.py:51
  2543.5 82.9 %collective-permute-start.67 = (f32[4,6,48,10,3,2]{2,0,5,4,3,1:T(4,128)}, f32[4,6,48,10,3,2]{2,0,5,4,3,1:T(4,128)}, u32[]{:S(2)}, u32[]{:S(2)}) collective-permute-start(f32[4,6,48,10,3,2]{2,0,5,4,3,1:T(4,128)} %copy.1059), channel_id=1, source_target_pairs={{0,1},{1,2},{2,3},{3,0},{4,5},{5,6},{6,7},{7,4},{8,9},{9,10},{10,1... | collective-permute-start | bytes 829448 | tf_op jit(solution)/shard_map/ppermute | solution.py:53
  2552.5 77.1 %collective-permute-start.69 = (f32[6,4,48,10,3,2]{2,1,5,4,3,0:T(4,128)}, f32[6,4,48,10,3,2]{2,1,5,4,3,0:T(4,128)}, u32[]{:S(2)}, u32[]{:S(2)}) collective-permute-start(f32[6,4,48,10,3,2]{2,1,5,4,3,0:T(4,128)} %fusion.791), channel_id=1, source_target_pairs={{0,4},{4,0},{1,5},{5,1},{2,6},{6,2},{3,7},{7,3},{8,12},{12,8},{9,1... | collective-permute-start | bytes 829448 | tf_op jit(solution)/shard_map/ppermute | solution.py:53
  2763.9 69.3 %collective-permute-start.72 = (f32[3,6,48,10,3,2]{2,5,4,3,1,0:T(2,128)}, f32[3,6,48,10,3,2]{2,5,4,3,1,0:T(2,128)}, u32[]{:S(2)}, u32[]{:S(2)}) collective-permute-start(f32[3,6,48,10,3,2]{2,5,4,3,1,0:T(2,128)} %copy.1106), channel_id=1, source_target_pairs={{0,3},{1,0},{2,1},{3,2},{4,7},{5,4},{6,5},{7,6},{8,11},{9,8},{10,9... | collective-permute-start | bytes 622088 | tf_op jit(solution)/shard_map/ppermute | solution.py:51
  2819.5 56.9 %collective-permute-start.77 = (f32[6,6,4,10,3,2]{3,2,5,4,1,0:T(4,128)S(1)}, f32[6,6,4,10,3,2]{3,2,5,4,1,0:T(4,128)S(1)}, u32[]{:S(2)}, u32[]{:S(2)}) collective-permute-start(f32[6,6,4,10,3,2]{3,2,5,4,1,0:T(4,128)S(1)} %pad_maximum_fusion.251), channel_id=1, source_target_pairs={{0,8},{8,16},{16,24},{24,0},{1,9},{9,17},{17,25},{25,1},{2,10},{10... | collective-permute-start | bytes 103688 | tf_op jit(solution)/shard_map/ppermute | solution.py:53
  2825.5 60.9 %collective-permute-start.75 = (f32[6,4,48,10,3,2]{2,1,5,4,3,0:T(4,128)}, f32[6,4,48,10,3,2]{2,1,5,4,3,0:T(4,128)}, u32[]{:S(2)}, u32[]{:S(2)}) collective-permute-start(f32[6,4,48,10,3,2]{2,1,5,4,3,0:T(4,128)} %fusion.787), channel_id=1, source_target_pairs={{0,4},{4,0},{1,5},{5,1},{2,6},{6,2},{3,7},{7,3},{8,12},{12,8},{9,1... | collective-permute-start | bytes 829448 | tf_op jit(solution)/shard_map/ppermute | solution.py:53
  2912.7 64.8 %collective-permute-start.80 = (f32[6,3,48,10,3,2]{2,5,4,3,1,0:T(2,128)}, f32[6,3,48,10,3,2]{2,5,4,3,1,0:T(2,128)}, u32[]{:S(2)}, u32[]{:S(2)}) collective-permute-start(f32[6,3,48,10,3,2]{2,5,4,3,1,0:T(2,128)} %copy.1188), channel_id=1, source_target_pairs={{0,4},{4,0},{1,5},{5,1},{2,6},{6,2},{3,7},{7,3},{8,12},{12,8},{9,1... | collective-permute-start | bytes 622088 | tf_op jit(solution)/shard_map/ppermute | solution.py:51
  2977.5 82.7 %collective-permute-start.79 = (f32[4,6,48,10,3,2]{2,0,5,4,3,1:T(4,128)}, f32[4,6,48,10,3,2]{2,0,5,4,3,1:T(4,128)}, u32[]{:S(2)}, u32[]{:S(2)}) collective-permute-start(f32[4,6,48,10,3,2]{2,0,5,4,3,1:T(4,128)} %copy.1185), channel_id=1, source_target_pairs={{0,1},{1,2},{2,3},{3,0},{4,5},{5,6},{6,7},{7,4},{8,9},{9,10},{10,1... | collective-permute-start | bytes 829448 | tf_op jit(solution)/shard_map/ppermute | solution.py:53
  2986.5 76.9 %collective-permute-start.81 = (f32[6,4,48,10,3,2]{2,1,5,4,3,0:T(4,128)}, f32[6,4,48,10,3,2]{2,1,5,4,3,0:T(4,128)}, u32[]{:S(2)}, u32[]{:S(2)}) collective-permute-start(f32[6,4,48,10,3,2]{2,1,5,4,3,0:T(4,128)} %fusion.783), channel_id=1, source_target_pairs={{0,4},{4,0},{1,5},{5,1},{2,6},{6,2},{3,7},{7,3},{8,12},{12,8},{9,1... | collective-permute-start | bytes 829448 | tf_op jit(solution)/shard_map/ppermute | solution.py:53
  3197.9 69.3 %collective-permute-start.84 = (f32[3,6,48,10,3,2]{2,5,4,3,1,0:T(2,128)}, f32[3,6,48,10,3,2]{2,5,4,3,1,0:T(2,128)}, u32[]{:S(2)}, u32[]{:S(2)}) collective-permute-start(f32[3,6,48,10,3,2]{2,5,4,3,1,0:T(2,128)} %copy.1232), channel_id=1, source_target_pairs={{0,3},{1,0},{2,1},{3,2},{4,7},{5,4},{6,5},{7,6},{8,11},{9,8},{10,9... | collective-permute-start | bytes 622088 | tf_op jit(solution)/shard_map/ppermute | solution.py:51
  3253.3 56.9 %collective-permute-start.89 = (f32[6,6,4,10,3,2]{3,2,5,4,1,0:T(4,128)S(1)}, f32[6,6,4,10,3,2]{3,2,5,4,1,0:T(4,128)S(1)}, u32[]{:S(2)}, u32[]{:S(2)}) collective-permute-start(f32[6,6,4,10,3,2]{3,2,5,4,1,0:T(4,128)S(1)} %pad_maximum_fusion.253), channel_id=1, source_target_pairs={{0,8},{8,16},{16,24},{24,0},{1,9},{9,17},{17,25},{25,1},{2,10},{10... | collective-permute-start | bytes 103688 | tf_op jit(solution)/shard_map/ppermute | solution.py:53
  3259.4 60.9 %collective-permute-start.87 = (f32[6,4,48,10,3,2]{2,1,5,4,3,0:T(4,128)}, f32[6,4,48,10,3,2]{2,1,5,4,3,0:T(4,128)}, u32[]{:S(2)}, u32[]{:S(2)}) collective-permute-start(f32[6,4,48,10,3,2]{2,1,5,4,3,0:T(4,128)} %fusion.779), channel_id=1, source_target_pairs={{0,4},{4,0},{1,5},{5,1},{2,6},{6,2},{3,7},{7,3},{8,12},{12,8},{9,1... | collective-permute-start | bytes 829448 | tf_op jit(solution)/shard_map/ppermute | solution.py:53
  3346.8 64.6 %collective-permute-start.92 = (f32[6,3,48,10,3,2]{2,5,4,3,1,0:T(2,128)}, f32[6,3,48,10,3,2]{2,5,4,3,1,0:T(2,128)}, u32[]{:S(2)}, u32[]{:S(2)}) collective-permute-start(f32[6,3,48,10,3,2]{2,5,4,3,1,0:T(2,128)} %copy.1314), channel_id=1, source_target_pairs={{0,4},{4,0},{1,5},{5,1},{2,6},{6,2},{3,7},{7,3},{8,12},{12,8},{9,1... | collective-permute-start | bytes 622088 | tf_op jit(solution)/shard_map/ppermute | solution.py:51
  3411.4 84.7 %collective-permute-start.91 = (f32[4,6,48,10,3,2]{2,0,5,4,3,1:T(4,128)}, f32[4,6,48,10,3,2]{2,0,5,4,3,1:T(4,128)}, u32[]{:S(2)}, u32[]{:S(2)}) collective-permute-start(f32[4,6,48,10,3,2]{2,0,5,4,3,1:T(4,128)} %copy.1311), channel_id=1, source_target_pairs={{0,1},{1,2},{2,3},{3,0},{4,5},{5,6},{6,7},{7,4},{8,9},{9,10},{10,1... | collective-permute-start | bytes 829448 | tf_op jit(solution)/shard_map/ppermute | solution.py:53
  3420.4 78.8 %collective-permute-start.93 = (f32[6,4,48,10,3,2]{2,1,5,4,3,0:T(4,128)}, f32[6,4,48,10,3,2]{2,1,5,4,3,0:T(4,128)}, u32[]{:S(2)}, u32[]{:S(2)}) collective-permute-start(f32[6,4,48,10,3,2]{2,1,5,4,3,0:T(4,128)} %fusion.775), channel_id=1, source_target_pairs={{0,4},{4,0},{1,5},{5,1},{2,6},{6,2},{3,7},{7,3},{8,12},{12,8},{9,1... | collective-permute-start | bytes 829448 | tf_op jit(solution)/shard_map/ppermute | solution.py:53
  (1091 other events, 7581.0 us)
where the time goes:
time: 3630 us; the launch traced here: 3610 us
  other arithmetic  1540 us (42%)
  local copies, waits for them, and re-layouts  1260 us (35%)
  blocking collectives  649 us (18%)
  starting transfers between devices  108 us (3%)
  between operations  49.5 us (1%)
    reduce_sum x128, other arithmetic, mat_vec(): jnp.sum(link_re * vec_re - link_im * vec_im, axis=-1)  585 us
    reduce_sum x16, other arithmetic, adj_vec(): jnp.sum(link_re * vec_re + link_im * vec_im, axis=-2)  417 us
    psum x8, blocking collectives, local_solve(): new_norm = lax.psum(jnp.sum(res_vec * res_vec), ALL_AXES)  333 us
    psum x7, blocking collectives, local_solve(): step_size = res_norm / lax.psum(jnp.sum(search_dir * applied), ALL_AXES)  277 us
    unnamed x2115, local copies, waits for them, and re-layouts  188 us
    reduce_sum x128, local copies, waits for them, and re-layouts, mat_vec(): jnp.sum(link_re * vec_im + link_im * vec_re, axis=-1)  138 us
    reduce_sum x128, local copies, waits for them, and re-layouts, mat_vec(): jnp.sum(link_re * vec_re - link_im * vec_im, axis=-1)  131 us
    mul x31, other arithmetic, mat_vec(): link_re * vec_re - link_im * vec_im  109 us

commit v1 on v0

v1 whole, which is shorter than its diff:
```python
import jax
import jax.numpy as jnp
from jax import lax
from jax.experimental import pallas as pl
from jax.experimental.pallas import tpu as pltpu
from jax.sharding import PartitionSpec as P

ITERS = 8
MESH = pl.DeviceIdType.MESH
F32 = jnp.float32
TL, ZL, YL, XH = 6, 6, 48, 10
R0 = 16
ROWS, LANES, HALF, VALID = 32, 128, 64, 30
XL = 5
NSTG = 4
COMPS, LINKS = range(6), range(18)
C0 = 3
STEPS = ((0, 1), (1, 3))
SITE = VALID * 2 * 6


def vec(*shape):
    return pltpu.VMEM(shape + (LANES,), F32)


def plane():
    return vec(ZL, 6, ROWS)


def sems(*shape):
    return pltpu.SemaphoreType.DMA(shape)


def halo_t():
    return vec(2, ZL, 6, R0)


def halo_y():
    return vec(2, ZL, ROWS)


SCRATCH = dict(
    lkt=vec(24, 18, 56), lko=vec(72, 18, ROWS), stg=pltpu.VMEM((2 * NSTG, 2304, YL), F32),
    f=vec(18, 6, 64), acc=plane(), cb=vec(2, 6, ROWS), xs=vec(2, 6, YL),
    r=plane(), p=plane(), s=plane(), z=plane(), x=plane(), zs=vec(2, 6, 136), zr=vec(2, 6, 136),
    tsf=halo_t(), trf=halo_t(), tsc=halo_t(), trc=halo_t(), ysf=halo_y(), yrf=halo_y(), ysc=halo_y(), yrc=halo_y(),
    rt=vec(2, 4, 6, 8), rz=vec(2, 2, 6, 8), ry=vec(2, 4, 6, 8), gd=vec(6, 8), cf=vec(8, 8),
    stg_sem=sems(NSTG, 12), io_sem=sems(36), z_ss=sems(2, 6), z_rs=sems(2, 6), h_ss=sems(2, 3, 4), h_rs=sems(2, 3, 4),
    a_ss=sems(2, 7), a_rs=sems(2, 7),
)


def mat(acc, link, psi):
    for i in range(3):
        for j in range(3):
            a, b = link(6 * i + 2 * j), link(6 * i + 2 * j + 1)
            c, d = psi[2 * j], psi[2 * j + 1]
            acc[2 * i] = acc[2 * i] + (a * c - b * d)
            acc[2 * i + 1] = acc[2 * i + 1] + (a * d + b * c)


def adj(acc, link, psi):
    for j in range(3):
        for i in range(3):
            a, b = link(6 * j + 2 * i), link(6 * j + 2 * i + 1)
            c, d = psi[2 * j], psi[2 * j + 1]
            acc[2 * i] = acc[2 * i] - (a * c + b * d)
            acc[2 * i + 1] = acc[2 * i + 1] + (b * c - a * d)


def rot(v, n):
    n %= LANES
    return pltpu.roll(v, n, 1) if n else v


def kernel(fat, lng, src, mass, out, res, *scratch):
    k = type('Refs', (), {})()
    for name, ref in zip(SCRATCH, scratch):
        setattr(k, name, ref)
    iy, iz, it = lax.axis_index('yy'), lax.axis_index('zz'), lax.axis_index('t')

    def at_t(d):
        return (iy, iz, lax.rem(it + d, 4))

    def at_z():
        return (iy, 1 - iz, it)

    def at_y(d):
        return (lax.rem(iy + d, 4), iz, it)

    def remote(src_ref, dst_ref, send, recv, dev):
        return pltpu.make_async_remote_copy(src_ref=src_ref, dst_ref=dst_ref, send_sem=send, recv_sem=recv, device_id=dev, device_id_type=MESH)

    others = range(1, 4)
    barrier = pltpu.get_barrier_semaphore()
    for dev in [at_t(d) for d in others] + [at_z()] + [at_y(d) for d in others]:
        pl.semaphore_signal(barrier, inc=1, device_id=dev, device_id_type=MESH)
    pl.semaphore_wait(barrier, 7)

    lane8, row8 = (lax.broadcasted_iota(jnp.int32, (8, LANES), d) for d in (1, 0))
    ylane8 = lane8 % HALF
    lane, row = (lax.broadcasted_iota(jnp.int32, (ROWS, LANES), d) for d in (1, 0))
    ylane, x5 = lane % HALF, lax.rem(row, XL)
    parity = row // XL + lane
    real = row < VALID
    good = real & (ylane < YL)
    seg0 = lane < HALF
    zero8 = jnp.zeros((8, LANES), F32)
    zeros = jnp.zeros((ROWS, LANES), F32)

    def lt(n, o, zi):
        return (n * 2 + o) * ZL + zi

    def lo(di, n, o, zi):
        return (((di - 1) * 2 + n) * 2 + o) * ZL + zi

    def field(i, j, c, off=0):
        return k.f[9 * i + j, c, pl.ds(R0 + off, ROWS), :]

    def psi_of(i, j, off=0):
        return [field(i, j, c, off) for c in COMPS]

    def each_src(act):
        for q in range(36):
            zi, ti = q // TL, q % TL
            act(q, pl.ds(zi * SITE + ti * 60, 60), ti, pl.ds(zi * 60, 60))

    def src_copy(q, here, ti, there):
        return pltpu.make_async_copy(src.at[ti, there], k.stg.at[0, here], k.io_sem.at[q])

    def out_copy(q, here, ti, there):
        return pltpu.make_async_copy(k.stg.at[0, here], out.at[ti, there], k.io_sem.at[q])

    def stg_copies(g):
        slot, di, zi = lax.rem(g, NSTG), g // ZL, lax.rem(g, ZL)
        return [pltpu.make_async_copy(ref.at[di, t, zi], k.stg.at[2 * slot + n, pl.ds(SITE * t, SITE)], k.stg_sem.at[slot, TL * n + t])
                for n, ref in enumerate((fat, lng)) for t in range(TL)]

    z16 = jnp.zeros((ROWS, R0), F32)

    def both(half):
        return jnp.where(real, jnp.concatenate([half[0], z16, half[1], z16], axis=1), 0.0)

    each_src(lambda *a: src_copy(*a).start())
    k.f[...] = jnp.zeros_like(k.f)
    for ref in (k.p, k.s, k.z, k.x):
        ref[...] = jnp.zeros_like(ref)
    k.lkt[:, :, 0:R0, :] = jnp.zeros((24, 18, R0, LANES), F32)
    k.lkt[:, :, R0 + ROWS:, :] = jnp.zeros((24, 18, 8, LANES), F32)
    each_src(lambda *a: src_copy(*a).wait())

    def src_plane(zi, _):
        for c in COMPS:
            v = both([k.stg[0, pl.ds(zi * SITE + 6 * s + c, ROWS, 12), :] for s in range(2)])
            k.f[zi, c, pl.ds(R0, ROWS), :] = v
            k.r[zi, c] = v
        return 0

    lax.fori_loop(0, ZL, src_plane, 0)

    def convert(g, ref, base, lead):
        slot, zi = lax.rem(g, NSTG), lax.rem(g, ZL)
        even = (((parity + zi) & 1) == 0)[:, 0:YL]

        def some_comps(q, _):
            for n in range(2):
                for u in range(3):
                    c = 3 * q + u
                    v = [[k.stg[2 * slot + n, pl.ds(c + (2 * s + h) * 18, ROWS, 72), :] for h in range(2)] for s in range(2)]
                    for o in range(2):
                        ref[lead(n, o, zi), c, pl.ds(base, ROWS), :] = both([jnp.where(even, v[s][o], v[s][1 - o]) for s in range(2)])
            return 0
        lax.fori_loop(0, 6, some_comps, 0)

    def load_step(g, ref, base, lead):
        for cp in stg_copies(g):
            cp.wait()
        convert(g, ref, base, lead)

        @pl.when(g + NSTG < 24)
        def _():
            for cp in stg_copies(g + NSTG):
                cp.start()

    for g in range(NSTG):
        for cp in stg_copies(jnp.int32(g)):
            cp.start()

    def load_t(g, _):
        load_step(g, k.lkt, R0, lt)
        return 0

    def load_o(g, _):
        load_step(g, k.lko, 0, lambda n, o, zi: lo(g // ZL, n, o, zi))
        return 0

    lax.fori_loop(0, ZL, load_t, 0)
    lax.fori_loop(ZL, 24, load_o, 0)

    def z_copy(i, m):
        return remote(k.zs.at[i, m], k.zr.at[i, m], k.z_ss.at[i, m], k.z_rs.at[i, m], at_z())

    def h_copies(i, t):
        pairs = ((k.tsf, k.trf, at_t(3)), (k.tsc, k.trc, at_t(1)), (k.ysf, k.yrf, at_y(3)), (k.ysc, k.yrc, at_y(1)))
        two = pl.ds(2 * t, 2)
        return [remote(a.at[i, two], b.at[i, two], k.h_ss.at[i, t, n], k.h_rs.at[i, t, n], dev) for n, (a, b, dev) in enumerate(pairs)]

    def plane_of(t, n2):
        first = jnp.where(t == 0, 1, jnp.where(t == 1, 0, 3))
        return first + n2 * jnp.where(t == 0, 3, 2)

    gap = ylane8 >= YL

    def rows_of(u, part, off=0):
        return pl.ds(off + 15 * (u % 2) + part, 8)

    def wire(host, part):
        return pl.ds(15 * host + part, 8)

    def pack(load, i, m):
        for u in range(3):
            for part in (0, 7):
                guest = load(9 + u, part)
                for q in range(3):
                    k.zs[i, m, wire(3 * q + u, part), :] = jnp.where(gap, rot(guest, YL - R0 * q), load(3 * q + u, part))

    def unpack(i, m, store):
        for u in range(3):
            for part in (0, 7):
                guest = zero8
                for q in range(3):
                    h = k.zr[i, m, wire(3 * q + u, part), :]
                    store(3 * q + u, part, jnp.where(gap, 0.0, h))
                    guest = jnp.where(ylane8 // R0 == q, rot(h, R0 * q - YL), guest)
                store(9 + u, part, guest)

    def start(i, *ms):
        for m in ms:
            z_copy(i, m).start()

    def arrive(i, *ms):
        for m in ms:
            z_copy(i, m).wait_recv()

    def pack_psi(i, m):
        pack(lambda u, part: k.f[9 * i + m, u // 2, rows_of(u, part, R0), :], i, m)

    def pack_c(i, m, b, *terms):
        acc = [zeros] * 6
        for n, j in terms:
            adj(acc, lambda c: k.lko[lo(1, n, i, j), c], psi_of(i, j))
        for c in COMPS:
            k.cb[b, c] = acc[c]
        pack(lambda u, part: k.cb[b, u // 2, rows_of(u, part), :], i, C0 + m)

    def unpack_psi(i, m):
        def store(u, part, v):
            k.f[9 * i + 6 + m, u // 2, rows_of(u, part, R0), :] = v
        unpack(i, m, store)

    def unpack_c(i, m):
        def store(u, part, v):
            w = jnp.where(row8 == 0, 0.0, v) if part else v
            k.acc[m, u // 2, rows_of(u, part), :] = k.acc[m, u // 2, rows_of(u, part), :] + w
        unpack(i, C0 + m, store)

    def send(i, t):
        @pl.when(t == 0)
        def _():
            pack_psi(i, 1)
            pack_c(i, 1, 0, (1, 4))
            start(i, 1, C0 + 1)

        @pl.when(t == 1)
        def _():
            pack_psi(i, 0)
            pack_psi(i, 2)
            start(i, 0, 2)

        @pl.when(t == 2)
        def _():
            pack_c(i, 0, 0, (0, 5), (1, 3))
            pack_c(i, 2, 1, (1, 5))
            start(i, C0, C0 + 2)

    def receive(i, t):
        @pl.when(t == 0)
        def _():
            arrive(i, 1, C0 + 1)
            unpack_psi(i, 1)
            unpack_c(i, 1)

        @pl.when(t == 1)
        def _():
            arrive(i, C0, C0 + 2)
            unpack_c(i, 0)
            unpack_c(i, 2)

        @pl.when(t == 2)
        def _():
            arrive(i, 0, 2)
            unpack_psi(i, 0)
            unpack_psi(i, 2)

    def post(i, t):
        o = 1 - i

        def one_plane(n2, _):
            j = plane_of(t, n2)
            slot = 2 * t + n2
            psi = psi_of(i, j)
            back = [zeros] * 6
            for n, off in STEPS:
                chi = [zeros] * 6
                adj(chi, lambda c: k.lko[lo(2, n, i, j), c], psi)
                back = [back[c] + rot(chi[c], off) for c in COMPS]
            fwd, bwd = psi[0], rot(back[0], -YL)
            for c in COMPS[1:]:
                here = ylane // 4 == c
                fwd = jnp.where(here, rot(psi[c], 4 * c), fwd)
                bwd = jnp.where(here, rot(back[c], 4 * c - YL), bwd)
            k.ysf[i, slot] = fwd
            k.ysc[i, slot] = bwd
            e = ((parity + (j + o)) & 1) == 1
            for n, _ in STEPS:
                chi = [zeros] * 6
                adj(chi, lambda c: k.lko[lo(3, n, i, j), c], psi)
                for c in COMPS:
                    k.xs[n, c, pl.ds(8, ROWS), :] = chi[c]
                    far = jnp.where(x5 > 0, k.xs[n, c, pl.ds(7, ROWS), :], k.xs[n, c, pl.ds(12, ROWS), :])
                    near = rot(jnp.where(seg0, chi[c], far), HALF)
                    back[c] = back[c] + (jnp.where(e, near, far) if n else jnp.where(e, chi[c], near))
            acc = back
            far = [jnp.where(x5 < 4, field(i, j, c, 1), field(i, j, c, -4)) for c in COMPS]
            near = [rot(jnp.where(seg0, far[c], psi[c]), HALF) for c in COMPS]
            mat(acc, lambda c: k.lko[lo(3, 0, o, j), c], [jnp.where(e, near[c], psi[c]) for c in COMPS])
            mat(acc, lambda c: k.lko[lo(3, 1, o, j), c], [jnp.where(e, far[c], near[c]) for c in COMPS])
            for n, off in STEPS:
                off *= XL
                adj(acc, lambda c: k.lkt[lt(n, i, j), c, pl.ds(R0 - off, ROWS), :], psi_of(i, j, -off))
            for c in COMPS:
                k.acc[j, c] = acc[c]
            for h in range(2):
                acc = [zero8] * 6
                for n, first in ((0, R0 + 25), (1, R0 + 15 + 8 * h)):
                    if n or not h:
                        adj(acc, lambda c: k.lkt[lt(n, i, j), c, pl.ds(first, 8), :], [k.f[9 * i + j, c, pl.ds(first, 8), :] for c in COMPS])
                for c in COMPS:
                    k.tsc[i, slot, c, pl.ds(8 * h, 8), :] = acc[c]
                    k.tsf[i, slot, c, pl.ds(8 * h, 8), :] = k.f[9 * i + j, c, pl.ds(R0 + 8 * h, 8), :]
            return 0

        lax.fori_loop(0, 2, one_plane, 0)
        for cp in h_copies(i, t):
            cp.start()

    m2 = mass[0] * mass[0]
    inside = pl.ds(R0, ROWS)

    def store_odd(j, acc):
        for c in COMPS:
            k.f[9 + j, c, inside, :] = acc[c]

    def update_even(j, acc):
        cw, aw, ax, beta = (jnp.broadcast_to(k.cf[v, 0:1], (ROWS, LANES)) for v in range(4))
        gg, dd = zeros, zeros
        for c in COMPS:
            w = jnp.where(real, k.f[j, c, inside, :], 0.0)
            n = m2 * w - acc[c]
            zv = n + beta * k.z[j, c]
            sv = w + beta * k.s[j, c]
            r = k.r[j, c]
            pv = r + beta * k.p[j, c]
            k.x[j, c] = k.x[j, c] + ax * pv
            r = r - ax * sv
            w = cw * w - aw * zv
            k.z[j, c], k.s[j, c], k.p[j, c], k.r[j, c], k.f[j, c, inside, :] = zv, sv, pv, r, w
            gg = gg + r * r
            dd = dd + w * r
        for v, t in enumerate((gg, dd)):
            k.gd[v] = k.gd[v] + sum(t[8 * b:8 * b + 8] for b in range(4))

    def finish(i, t, update):
        o = 1 - i
        for cp in h_copies(i, t):
            cp.wait_recv()

        def one_plane(n2, _):
            j = plane_of(t, n2)
            slot = 2 * t + n2
            for c in COMPS:
                k.f[9 * i + j, c, pl.ds(R0 + VALID, R0), :] = k.trf[i, slot, c]
            yf, yc = k.yrf[i, slot], k.yrc[i, slot]
            top = (ylane >= YL) & (ylane < YL + 3)
            psi = [jnp.where(top, rot(yf, YL - 4 * c), field(i, j, c)) for c in COMPS]
            low = [jnp.where(ylane < 3, rot(yc, -4 * c), 0.0) for c in COMPS]
            acc = [k.acc[j, c] + low[c] for c in COMPS]
            for n, off in STEPS:
                mat(acc, lambda c: k.lkt[lt(n, o, j), c, inside, :], psi_of(i, j, XL * off))
            for n, off in STEPS:
                mat(acc, lambda c: k.lko[lo(1, n, o, j), c], psi_of(i, j + off))
                jb, on = jnp.maximum(j - off, 0), jnp.where(j >= off, 1.0, 0.0)
                adj(acc, lambda c: k.lko[lo(1, n, i, jb), c], [on * v for v in psi_of(i, jb)])
            for n, off in STEPS:
                mat(acc, lambda c: k.lko[lo(2, n, o, j), c], [rot(psi[c], -off) for c in COMPS])
            extra = [jnp.concatenate([k.trc[i, slot, c], zeros[:R0]], axis=0) for c in COMPS]
            update(j, [jnp.where(good, acc[c] + extra[c], 0.0) for c in COMPS])
            return 0

        lax.fori_loop(0, 2, one_plane, 0)

    def a_copies(stage, b, n):
        buf, me, first = ((k.rt, it, -1), (k.rz, iz, 3), (k.ry, iy, 3))[stage]
        to = ([at_t(d) for d in others], [at_z()], [at_y(d) for d in others])[stage]
        mine = buf.at[b, me, pl.ds(0, n)]
        first = (0, 3, 4)[stage]
        return [remote(mine, mine, k.a_ss.at[b, first + d], k.a_rs.at[b, first + d], dev) for d, dev in enumerate(to)]

    def sum_start(b, n):
        for v in range(n):
            k.rt[b, it, v] = k.gd[v]
        for cp in a_copies(0, b, n):
            cp.start()

    def sum_next(stage, b, n):
        for cp in a_copies(stage, b, n):
            cp.wait()
        frm = (k.rt, k.rz, k.ry)[stage]
        for v in range(n):
            tot = frm[b, 0, v] + frm[b, 1, v]
            if stage != 1:
                tot = tot + frm[b, 2, v] + frm[b, 3, v]
            if stage == 0:
                k.rz[b, iz, v] = tot
            elif stage == 1:
                k.ry[b, iy, v] = tot
            else:
                k.gd[v] = jnp.broadcast_to(jnp.sum(jnp.sum(tot, axis=0, keepdims=True), axis=1, keepdims=True), (8, LANES))
        if stage < 2:
            for cp in a_copies(stage + 1, b, n):
                cp.start()

    CW, AW, AX, BETA, GAMMA, ALPHA, FIRST = range(7)
    one = jnp.ones((8, LANES), F32)
    for v, t in ((CW, zero8), (AW, -one), (AX, zero8), (BETA, zero8), (GAMMA, one), (ALPHA, one)):
        k.cf[v] = t

    def scalars(step):
        gamma, delta = k.gd[0], k.gd[1]

        @pl.when(step == 1)
        def _():
            k.cf[ALPHA] = gamma / delta
            k.cf[FIRST] = gamma

        @pl.when(step > 1)
        def _():
            beta = gamma / k.cf[GAMMA]
            k.cf[BETA] = beta
            k.cf[ALPHA] = gamma / (delta - beta * gamma / k.cf[ALPHA])
            res[step - 2] = (gamma / k.cf[FIRST])[0, 0]
        k.cf[CW], k.cf[AW], k.cf[AX], k.cf[GAMMA] = one, k.cf[ALPHA], k.cf[ALPHA], gamma

    def phase(u, _):
        n, ph = u // 3 - 1, lax.rem(u, 3)
        i = lax.rem(n + 2, 2)
        step = n // 2
        b = lax.rem(jnp.maximum(step, 0), 2)
        t = jnp.where(ph == 0, 0, jnp.where((ph == 1) == (i == 0), 1, 2))
        live = n >= 0
        summing = (step > 0) & live

        @pl.when(summing & (i == 0) & (ph == 1))
        def _():
            sum_next(0, b, 2)

        @pl.when(summing & (i == 0) & (ph == 2))
        def _():
            sum_next(1, b, 2)

        @pl.when(live & (i == 1) & (ph == 0))
        def _():
            @pl.when(step > 0)
            def _():
                sum_next(2, b, 2)
                scalars(step)
            k.gd[0], k.gd[1] = zero8, zero8

        @pl.when(live)
        def _():
            receive(i, t)

            @pl.when(i == 0)
            def _():
                finish(0, t, store_odd)

            @pl.when(i == 1)
            def _():
                finish(1, t, update_even)

        @pl.when(n < 2 * ITERS - 1)
        def _():
            send(1 - i, t)
            post(1 - i, t)

        @pl.when(live & (ph == 2))
        def _():
            for m in range(6):
                z_copy(i, m).wait_send()
            for g in range(3):
                for cp in h_copies(i, g):
                    cp.wait_send()

            @pl.when((i == 1) & (step < ITERS - 1))
            def _():
                sum_start(1 - b, 2)
        return 0

    lax.fori_loop(0, 3 * (2 * ITERS + 1), phase, 0)

    def dots(j, carry):
        for c in COMPS:
            w, r, s = k.f[j, c, inside, :], k.r[j, c], k.s[j, c]
            carry = tuple(t + u * v for t, (u, v) in zip(carry, ((r, r), (w, r), (w, w), (r, s), (w, s), (s, s))))
        return carry

    for v, t in enumerate(lax.fori_loop(0, ZL, dots, (zeros,) * 6)):
        k.gd[v] = sum(t[8 * b:8 * b + 8] for b in range(4))
    sum_start(0, 6)
    for stage in range(3):
        sum_next(stage, 0, 6)
    rr, wr, ww, rs, ws, ss = (k.gd[v] for v in range(6))
    beta = rr / k.cf[GAMMA]
    alpha = rr / (wr - beta * rr / k.cf[ALPHA])
    last = rr - 2.0 * alpha * (wr + beta * rs) + alpha * alpha * (ww + 2.0 * beta * ws + beta * beta * ss)
    for v, t in ((ITERS - 2, rr), (ITERS - 1, last)):
        res[v] = (t / k.cf[FIRST])[0, 0]
    alpha, beta = (jnp.broadcast_to(v[0:1], (ROWS, LANES)) for v in (alpha, beta))

    def out_plane(j, _):
        for c in COMPS:
            v = k.x[j, c] + alpha * (k.r[j, c] + beta * k.p[j, c])
            for s in range(2):
                k.stg[0, pl.ds(j * SITE + 6 * s + c, VALID, 12), :] = rot(v, HALF * s)[0:VALID, 0:YL]
        return 0

    lax.fori_loop(0, ZL, out_plane, 0)
    each_src(lambda *a: out_copy(*a).start())
    each_src(lambda *a: out_copy(*a).wait())


def solution(mesh):
    link_spec = P(None, 't', 'zz', 'yy', None, None, None, None)
    field_spec = P('t', 'zz', 'yy', None, None, None)

    def local_solve(fat_links, long_links, source, quark_mass):
        fat, lng = (jnp.transpose(v, (0, 1, 2, 4, 5, 6, 7, 3)).reshape(4, TL, ZL, SITE, YL) for v in (fat_links, long_links))
        src = jnp.transpose(source, (0, 1, 3, 4, 5, 2)).reshape(TL, SITE, YL)
        anywhere, scalar = (pl.BlockSpec(memory_space=space) for space in (pl.ANY, pltpu.SMEM))
        sol, res = pl.pallas_call(
            kernel,
            out_shape=tuple(jax.ShapeDtypeStruct(shape, F32) for shape in ((TL, SITE, YL), (8,))),
            in_specs=[anywhere] * 3 + [scalar],
            out_specs=(anywhere, scalar),
            scratch_shapes=list(SCRATCH.values()),
            compiler_params=pltpu.CompilerParams(collective_id=0, has_side_effects=True, vmem_limit_bytes=67043328),
            name='cg',
        )(fat, lng, src, quark_mass)
        return jnp.transpose(sol.reshape(TL, ZL, XH, 3, 2, YL), (0, 1, 5, 2, 3, 4)), res

    return jax.shard_map(local_solve, mesh=mesh, in_specs=(link_spec, link_spec, field_spec, P(None)), out_specs=(field_spec, P()), check_vma=False)
```

time: 3630 us -> 203 us (0.06)
  other arithmetic: 1540 us -> 0 us
  local copies, waits for them, and re-layouts: 1260 us -> 3.13 us
  blocking collectives: 649 us -> 0 us
  Pallas kernels: 0 us -> 198 us
  starting transfers between devices: 108 us -> 0 us
  between operations: 49.5 us -> 1.29 us
    reduce_sum x161 -> x0, other arithmetic: 1120 us -> none  [the longest x128 585 us: mat_vec(): jnp.sum(link_re * vec_re - link_im * vec_im, axis=-1)]
    psum x16 -> x0, blocking collectives: 649 us -> none  [the longest x8 333 us: local_solve(): new_norm = lax.psum(jnp.sum(res_vec * res_vec), ALL_AXES)]
    reduce_sum x512 -> x0, local copies, waits for them, and re-layouts: 408 us -> none  [the longest x128 138 us: mat_vec(): jnp.sum(link_re * vec_im + link_im * vec_re, axis=-1)]
    slice x289 -> x0, local copies, waits for them, and re-layouts: 317 us -> none  [the longest x77 91.6 us: cut_shifts(): lax.slice_in_dim(psi_in, 0, 3, axis=axis_dim)]
    pallas_call x0 -> x1, Pallas kernels: none -> 198 us  [local_solve(): pl.pallas_call(kernel, out_shape=tuple((jax.ShapeDtypeStruct(shape, F32)...]
    unnamed x2115 -> x4, local copies, waits for them, and re-layouts: 188 us -> 3.13 us
    mul x321 -> x0, local copies, waits for them, and re-layouts: 173 us -> none  [the longest x161 78.3 us: mat_vec(): link_re * vec_re - link_im * vec_im]
    mul x31 -> x0, other arithmetic: 109 us -> none  [mat_vec(): link_re * vec_re - link_im * vec_im]
where the time goes in v1:
time: 203 us
  Pallas kernels  198 us (98%)
  local copies, waits for them, and re-layouts  3.13 us (2%)
    pallas_call x1, Pallas kernels, local_solve(): pl.pallas_call(kernel, out_shape=tuple((jax.ShapeDtypeStruct(shape, F32)...  198 us

profile of v1, /device:TPU:0, one launch (start us, length us, event | category | flops | bytes accessed | tf_op | source)
XLA Modules:
  0.0 202.7 jit_solution(10224774608755647130)
XLA Ops:
  1.3 198.3 %cg.1 = (f32[6,360,48]{2,1,0:T(8,128)}, f32[8]{0:T(128)}) custom-call(f32[4,6,6,360,48]{4,3,2,1,0:T(8,128)} %bitcast.12, f32[4,6,6,360,48]{4,3,2,1,0:T(8,128)} %bitcast.13, f32[6,360,48]{2,1,0:T(8,128)} %bitcast.14, f32[1]{0:T(128)S(6)} %copy.8.mass), custom_call_target="tpu_custom_call" | custom-call | tf_op jit(solution)/shard_map/cg/pallas_call | solution.py:560
  199.6 0.0 copy-start
  199.6 2.6 %copy.9 = f32[6,6,48,10,3,2]{2,5,4,3,1,0:T(2,128)} copy(f32[6,6,48,10,3,2]{2,5,4,3,1,0:T(2,128)} %bitcast.15) | data formatting | bytes 829440
  202.2 0.0 copy-done
  202.2 0.5 copy.10
Async XLA Ops:
  199.6 2.6 %copy-start = (f32[8]{0:T(128)S(1)}, f32[8]{0:T(128)}, u32[]{:S(2)}) copy-start(f32[8]{0:T(128)} %get-tuple-element.9) | copy-start | bytes 100

commit v2 on v1

v2 whole, which is shorter than its diff:
```python
import jax
import jax.numpy as jnp
from jax import lax
from jax.experimental import pallas as pl
from jax.experimental.pallas import tpu as pltpu
from jax.sharding import PartitionSpec as P

ITERS = 8
MESH = pl.DeviceIdType.MESH
F32 = jnp.float32
TL, ZL, YL, XH = 6, 6, 48, 10
R0 = 16
ROWS, LANES, HALF, VALID = 32, 128, 64, 30
XL = 5
NSTG = 4
COMPS, LINKS = range(6), range(18)
C0 = 3
STEPS = ((0, 1), (1, 3))
SITE = VALID * 2 * 6
LOADS = 4 * ZL
BLK = 16
BLOCKS = range(0, ROWS, BLK)


def vec(*shape):
    return pltpu.VMEM(shape + (LANES,), F32)


def plane():
    return vec(ZL, 6, ROWS)


def sems(*shape):
    return pltpu.SemaphoreType.DMA(shape)


def halo_t():
    return vec(2, ZL, 6, R0)


def halo_y():
    return vec(2, ZL, BLK)


SCRATCH = dict(
    lkt=vec(24, 18, 56), lko=vec(72, 18, ROWS), stg=pltpu.VMEM((2 * NSTG, 2304, YL), F32), sst=pltpu.VMEM((2304, YL), F32),
    f=vec(18, 6, 64), acc=plane(), cb=vec(2, 6, ROWS), xs=vec(2, 6, YL),
    r=plane(), p=plane(), s=plane(), z=plane(), x=plane(), zs=vec(2, 6, 136), zr=vec(2, 6, 136),
    tsf=halo_t(), trf=halo_t(), tsc=halo_t(), trc=halo_t(), ysf=halo_y(), yrf=halo_y(), ysc=halo_y(), yrc=halo_y(),
    ra=vec(2, 8, 8), rb=vec(2, 4, 8), gd=vec(6, 8), cf=vec(8, 8),
    stg_sem=sems(NSTG, 12), io_sem=sems(36), z_ss=sems(2, 6), z_rs=sems(2, 6), h_ss=sems(2, 3, 4), h_rs=sems(2, 3, 4),
    a_ss=sems(2, 10), a_rs=sems(2, 10),
)


def mat(acc, link, psi):
    for i in range(3):
        for j in range(3):
            a, b = link(6 * i + 2 * j), link(6 * i + 2 * j + 1)
            c, d = psi[2 * j], psi[2 * j + 1]
            acc[2 * i] = acc[2 * i] + (a * c - b * d)
            acc[2 * i + 1] = acc[2 * i + 1] + (a * d + b * c)


def adj(acc, link, psi):
    for j in range(3):
        for i in range(3):
            a, b = link(6 * j + 2 * i), link(6 * j + 2 * i + 1)
            c, d = psi[2 * j], psi[2 * j + 1]
            acc[2 * i] = acc[2 * i] - (a * c + b * d)
            acc[2 * i + 1] = acc[2 * i + 1] + (b * c - a * d)


def rot(v, n):
    n %= LANES
    return pltpu.roll(v, n, 1) if n else v


def kernel(fat, lng, src, mass, out, res, *scratch):
    k = type('Refs', (), {})()
    for name, ref in zip(SCRATCH, scratch):
        setattr(k, name, ref)
    iy, iz, it = lax.axis_index('yy'), lax.axis_index('zz'), lax.axis_index('t')

    def at_t(d):
        return (iy, iz, lax.rem(it + d, 4))

    def at_z(d=0):
        return (iy, 1 - iz, lax.rem(it + d, 4))

    def at_y(d):
        return (lax.rem(iy + d, 4), iz, it)

    def remote(src_ref, dst_ref, send, recv, dev):
        return pltpu.make_async_remote_copy(src_ref=src_ref, dst_ref=dst_ref, send_sem=send, recv_sem=recv, device_id=dev, device_id_type=MESH)

    others = range(1, 4)
    near = [at_t(d) for d in others] + [at_z(d) for d in range(4)]
    ring = [at_y(d) for d in others]

    def plane_of(t, n2):
        first = jnp.where(t == 0, 1, jnp.where(t == 1, 0, 3))
        return first + n2 * jnp.where(t == 0, 3, 2)

    def what(g):
        q = jnp.maximum(g - ZL, 0)
        d = lax.rem(q, 3)
        p = q // 3
        early = g < ZL
        return jnp.where(early, 1, jnp.where(d == 0, 0, d + 1)), jnp.where(early, g, plane_of(p // 2, lax.rem(p, 2)))

    def stg_copies(g):
        slot = lax.rem(g, NSTG)
        di, zi = what(g)
        return [pltpu.make_async_copy(ref.at[di, t, zi], k.stg.at[2 * slot + n, pl.ds(SITE * t, SITE)], k.stg_sem.at[slot, TL * n + t])
                for n, ref in enumerate((fat, lng)) for t in range(TL)]

    def each_src(act):
        for q in range(TL * ZL):
            zi, ti = q // TL, q % TL
            act(q, pl.ds(zi * SITE + ti * 60, 60), ti, pl.ds(zi * 60, 60))

    def src_copy(q, here, ti, there):
        return pltpu.make_async_copy(src.at[ti, there], k.sst.at[here], k.io_sem.at[q])

    def out_copy(q, here, ti, there):
        return pltpu.make_async_copy(k.sst.at[here], out.at[ti, there], k.io_sem.at[q])

    barrier = pltpu.get_barrier_semaphore()
    for dev in near + ring:
        pl.semaphore_signal(barrier, inc=1, device_id=dev, device_id_type=MESH)
    each_src(lambda *a: src_copy(*a).start())
    for g in range(NSTG):
        for cp in stg_copies(jnp.int32(g)):
            cp.start()

    lane8, row8 = (lax.broadcasted_iota(jnp.int32, (8, LANES), d) for d in (1, 0))
    ylane8 = lane8 % HALF
    lane, row = (lax.broadcasted_iota(jnp.int32, (ROWS, LANES), d) for d in (1, 0))
    lane_b, row_b = lane[:BLK], row[:BLK]
    ylane = lane_b % HALF
    seg0 = lane_b < HALF
    zero8 = jnp.zeros((8, LANES), F32)
    zeros = jnp.zeros((BLK, LANES), F32)

    def lt(n, o, zi):
        return (n * 2 + o) * ZL + zi

    def lo(di, n, o, zi):
        return (((di - 1) * 2 + n) * 2 + o) * ZL + zi

    def at(h, off=0):
        return pl.ds(off + h, BLK)

    def psi_of(i, j, h, off=0):
        return [k.f[9 * i + j, c, at(h, R0 + off), :] for c in COMPS]

    k.f[...] = jnp.zeros_like(k.f)
    for ref in (k.p, k.s, k.z, k.x):
        ref[...] = jnp.zeros_like(ref)
    k.lkt[:, :, 0:R0, :] = jnp.zeros((24, 18, R0, LANES), F32)
    k.lkt[:, :, R0 + ROWS:, :] = jnp.zeros((24, 18, 8, LANES), F32)

    z16 = jnp.zeros((ROWS, R0), F32)

    def both(half):
        return jnp.where(row < VALID, jnp.concatenate([half[0], z16, half[1], z16], axis=1), 0.0)

    def src_plane(zi, _):
        for c in COMPS:
            v = both([k.sst[pl.ds(zi * SITE + 6 * s + c, ROWS, 12), :] for s in range(2)])
            k.f[zi, c, pl.ds(R0, ROWS), :] = v
            k.r[zi, c] = v
        return 0

    each_src(lambda *a: src_copy(*a).wait())
    lax.fori_loop(0, ZL, src_plane, 0)
    pl.semaphore_wait(barrier, len(near + ring))

    def convert(g, zi, ref, base, lead):
        slot = lax.rem(g, NSTG)
        even = (((row // XL + lane + zi) & 1) == 0)[:, 0:YL]

        def some_comps(q, _):
            for n in range(2):
                for u in range(3):
                    c = 3 * q + u
                    v = [[k.stg[2 * slot + n, pl.ds(c + (2 * s + h) * 18, ROWS, 72), :] for h in range(2)] for s in range(2)]
                    for o in range(2):
                        ref[lead(n, o, zi), c, pl.ds(base, ROWS), :] = both([jnp.where(even, v[s][o], v[s][1 - o]) for s in range(2)])
            return 0
        lax.fori_loop(0, 6, some_comps, 0)

    def load_step(g, _):
        di, zi = what(g)
        for cp in stg_copies(g):
            cp.wait()

        @pl.when(di == 0)
        def _():
            convert(g, zi, k.lkt, R0, lt)

        @pl.when(di > 0)
        def _():
            convert(g, zi, k.lko, 0, lambda n, o, zi: lo(di, n, o, zi))

        @pl.when(g + NSTG < LOADS)
        def _():
            for cp in stg_copies(g + NSTG):
                cp.start()
        return 0

    def z_copy(i, m):
        return remote(k.zs.at[i, m], k.zr.at[i, m], k.z_ss.at[i, m], k.z_rs.at[i, m], at_z())

    def h_copies(i, t):
        pairs = ((k.tsf, k.trf, at_t(3)), (k.tsc, k.trc, at_t(1)), (k.ysf, k.yrf, at_y(3)), (k.ysc, k.yrc, at_y(1)))
        two = pl.ds(2 * t, 2)
        return [remote(a.at[i, two], b.at[i, two], k.h_ss.at[i, t, n], k.h_rs.at[i, t, n], dev) for n, (a, b, dev) in enumerate(pairs)]

    gap = ylane8 >= YL

    def rows_of(u, part, off=0):
        return pl.ds(off + 15 * (u % 2) + part, 8)

    def wire(host, part):
        return pl.ds(15 * host + part, 8)

    def pack(load, i, m):
        for u in range(3):
            for part in (0, 7):
                guest = load(9 + u, part)
                for q in range(3):
                    k.zs[i, m, wire(3 * q + u, part), :] = jnp.where(gap, rot(guest, YL - R0 * q), load(3 * q + u, part))

    def unpack(i, m, store):
        for u in range(3):
            for part in (0, 7):
                guest = zero8
                for q in range(3):
                    h = k.zr[i, m, wire(3 * q + u, part), :]
                    store(3 * q + u, part, jnp.where(gap, 0.0, h))
                    guest = jnp.where(ylane8 // R0 == q, rot(h, R0 * q - YL), guest)
                store(9 + u, part, guest)

    def start(i, *ms):
        for m in ms:
            z_copy(i, m).start()

    def arrive(i, *ms):
        for m in ms:
            z_copy(i, m).wait_recv()

    def pack_psi(i, m):
        pack(lambda u, part: k.f[9 * i + m, u // 2, rows_of(u, part, R0), :], i, m)

    def pack_c(i, m, b, *terms):
        for h in BLOCKS:
            acc = [zeros] * 6
            for n, j in terms:
                adj(acc, lambda c: k.lko[lo(1, n, i, j), c, at(h), :], psi_of(i, j, h))
            for c in COMPS:
                k.cb[b, c, at(h), :] = acc[c]
        pack(lambda u, part: k.cb[b, u // 2, rows_of(u, part), :], i, C0 + m)

    def unpack_psi(i, m):
        def store(u, part, v):
            k.f[9 * i + 6 + m, u // 2, rows_of(u, part, R0), :] = v
        unpack(i, m, store)

    def unpack_c(i, m):
        def store(u, part, v):
            w = jnp.where(row8 == 0, 0.0, v) if part else v
            k.acc[m, u // 2, rows_of(u, part), :] = k.acc[m, u // 2, rows_of(u, part), :] + w
        unpack(i, C0 + m, store)

    def send(i, t):
        @pl.when(t == 0)
        def _():
            pack_psi(i, 1)
            pack_c(i, 1, 0, (1, 4))
            start(i, 1, C0 + 1)

        @pl.when(t == 1)
        def _():
            pack_psi(i, 0)
            pack_psi(i, 2)
            start(i, 0, 2)

        @pl.when(t == 2)
        def _():
            pack_c(i, 0, 0, (0, 5), (1, 3))
            pack_c(i, 2, 1, (1, 5))
            start(i, C0, C0 + 2)

    def receive(i, t):
        @pl.when(t == 0)
        def _():
            arrive(i, 1, C0 + 1)
            unpack_psi(i, 1)
            unpack_c(i, 1)

        @pl.when(t == 1)
        def _():
            arrive(i, C0, C0 + 2)
            unpack_c(i, 0)
            unpack_c(i, 2)

        @pl.when(t == 2)
        def _():
            arrive(i, 0, 2)
            unpack_psi(i, 0)
            unpack_psi(i, 2)

    def tell(i, t):
        def one_plane(n2, _):
            j = plane_of(t, n2)
            slot = 2 * t + n2
            fwd, bwd = zeros, zeros
            for h in BLOCKS:
                psi = psi_of(i, j, h)
                back = [zeros] * 6
                for n, off in STEPS:
                    chi = [zeros] * 6
                    adj(chi, lambda c: k.lko[lo(2, n, i, j), c, at(h), :], psi)
                    back = [back[c] + rot(chi[c], off) for c in COMPS]
                for c in COMPS:
                    k.acc[j, c, at(h), :] = back[c]
                    to = 4 * c + 24 * (h // BLK)
                    here = ylane // 4 == to // 4
                    fwd = jnp.where(here, rot(psi[c], to), fwd)
                    bwd = jnp.where(here, rot(back[c], to - YL), bwd)
            k.ysf[i, slot] = fwd
            k.ysc[i, slot] = bwd
            for h in range(2):
                acc = [zero8] * 6
                for n, first in ((0, R0 + 25), (1, R0 + 15 + 8 * h)):
                    if n or not h:
                        adj(acc, lambda c: k.lkt[lt(n, i, j), c, pl.ds(first, 8), :], [k.f[9 * i + j, c, pl.ds(first, 8), :] for c in COMPS])
                for c in COMPS:
                    k.tsc[i, slot, c, pl.ds(8 * h, 8), :] = acc[c]
                    k.tsf[i, slot, c, pl.ds(8 * h, 8), :] = k.f[9 * i + j, c, pl.ds(R0 + 8 * h, 8), :]
            return 0

        lax.fori_loop(0, 2, one_plane, 0)
        for cp in h_copies(i, t):
            cp.start()

    def post(i, t):
        o = 1 - i

        def one_plane(n2, _):
            j = plane_of(t, n2)
            for h in BLOCKS:
                psi = psi_of(i, j, h)
                for n, _ in STEPS:
                    chi = [zeros] * 6
                    adj(chi, lambda c: k.lko[lo(3, n, i, j), c, at(h), :], psi)
                    for c in COMPS:
                        k.xs[n, c, at(h, 8), :] = chi[c]
            for h in BLOCKS:
                x5 = lax.rem(row_b + h, XL)
                e = (((row_b + h) // XL + lane_b + (j + o)) & 1) == 1
                acc = [k.acc[j, c, at(h), :] for c in COMPS]
                for n, _ in STEPS:
                    for c in COMPS:
                        own = k.xs[n, c, at(h, 8), :]
                        far = jnp.where(x5 > 0, k.xs[n, c, at(h, 7), :], k.xs[n, c, at(h, 12), :])
                        close = rot(jnp.where(seg0, own, far), HALF)
                        acc[c] = acc[c] + (jnp.where(e, close, far) if n else jnp.where(e, own, close))
                for n, off in STEPS:
                    off *= XL
                    adj(acc, lambda c: k.lkt[lt(n, i, j), c, at(h, R0 - off), :], psi_of(i, j, h, -off))
                psi = psi_of(i, j, h)
                far = [jnp.where(x5 < 4, u, v) for u, v in zip(psi_of(i, j, h, 1), psi_of(i, j, h, -4))]
                close = [rot(jnp.where(seg0, far[c], psi[c]), HALF) for c in COMPS]
                mat(acc, lambda c: k.lko[lo(3, 0, o, j), c, at(h), :], [jnp.where(e, close[c], psi[c]) for c in COMPS])
                mat(acc, lambda c: k.lko[lo(3, 1, o, j), c, at(h), :], [jnp.where(e, far[c], close[c]) for c in COMPS])
                for c in COMPS:
                    k.acc[j, c, at(h), :] = acc[c]
            return 0

        lax.fori_loop(0, 2, one_plane, 0)

    m2 = mass[0] * mass[0]

    def store_odd(j, h, real, acc):
        for c in COMPS:
            k.f[9 + j, c, at(h, R0), :] = acc[c]

    def update_even(j, h, real, acc):
        cw, aw, ax, beta = (jnp.broadcast_to(k.cf[v, 0:1], (BLK, LANES)) for v in range(4))
        gg, dd = zeros, zeros
        for c in COMPS:
            sl, fl = (j, c, at(h), slice(None)), (j, c, at(h, R0), slice(None))
            w = jnp.where(real, k.f[fl], 0.0)
            n = m2 * w - acc[c]
            zv = n + beta * k.z[sl]
            sv = w + beta * k.s[sl]
            r = k.r[sl]
            pv = r + beta * k.p[sl]
            k.x[sl] = k.x[sl] + ax * pv
            r = r - ax * sv
            w = cw * w - aw * zv
            k.z[sl], k.s[sl], k.p[sl], k.r[sl], k.f[fl] = zv, sv, pv, r, w
            gg = gg + r * r
            dd = dd + w * r
        for v, t in enumerate((gg, dd)):
            k.gd[v] = k.gd[v] + (t[:8] + t[8:])

    def finish(i, t, update):
        o = 1 - i
        for cp in h_copies(i, t):
            cp.wait_recv()

        def one_plane(n2, _):
            j = plane_of(t, n2)
            slot = 2 * t + n2
            for c in COMPS:
                k.f[9 * i + j, c, pl.ds(R0 + VALID, R0), :] = k.trf[i, slot, c]
            yf, yc = k.yrf[i, slot], k.yrc[i, slot]
            for h in BLOCKS:
                frm = [4 * c + 24 * (h // BLK) for c in COMPS]
                top = (ylane >= YL) & (ylane < YL + 3)
                psi = [jnp.where(top, rot(yf, YL - frm[c]), v) for c, v in enumerate(psi_of(i, j, h))]
                acc = [k.acc[j, c, at(h), :] + jnp.where(ylane < 3, rot(yc, -frm[c]), 0.0) for c in COMPS]
                if h == 0:
                    acc = [acc[c] + k.trc[i, slot, c] for c in COMPS]
                for n, off in STEPS:
                    mat(acc, lambda c: k.lkt[lt(n, o, j), c, at(h, R0), :], psi_of(i, j, h, XL * off))
                for n, off in STEPS:
                    mat(acc, lambda c: k.lko[lo(1, n, o, j), c, at(h), :], psi_of(i, j + off, h))
                    jb, on = jnp.maximum(j - off, 0), jnp.where(j >= off, 1.0, 0.0)
                    adj(acc, lambda c: k.lko[lo(1, n, i, jb), c, at(h), :], [on * v for v in psi_of(i, jb, h)])
                for n, off in STEPS:
                    mat(acc, lambda c: k.lko[lo(2, n, o, j), c, at(h), :], [rot(psi[c], -off) for c in COMPS])
                real = row_b + h < VALID
                good = real & (ylane < YL)
                update(j, h, real, [jnp.where(good, acc[c], 0.0) for c in COMPS])
            return 0

        lax.fori_loop(0, 2, one_plane, 0)

    def a_copies(stage, b):
        mine = k.rb.at[b, iy] if stage else k.ra.at[b, 4 * iz + it]
        return [remote(mine, mine, k.a_ss.at[b, d], k.a_rs.at[b, d], dev) for d, dev in enumerate(near + ring) if (d >= len(near)) == bool(stage)]

    def sum_start(b, n):
        tile = zero8
        for v in range(n):
            tile = jnp.where(row8 == v, jnp.sum(k.gd[v], axis=0, keepdims=True), tile)
        k.ra[b, 4 * iz + it] = tile
        for cp in a_copies(0, b):
            cp.start()

    def sum_next(b):
        for cp in a_copies(0, b):
            cp.wait()
        k.rb[b, iy] = sum(k.ra[b, d] for d in range(1, 8)) + k.ra[b, 0]
        for cp in a_copies(1, b):
            cp.start()

    def sum_end(b, n):
        for cp in a_copies(1, b):
            cp.wait()
        tile = sum(k.rb[b, d] for d in others) + k.rb[b, 0]
        tile = jnp.broadcast_to(jnp.sum(tile, axis=1, keepdims=True), (8, LANES))
        return [jnp.broadcast_to(tile[v:v + 1], (8, LANES)) for v in range(n)]

    CW, AW, AX, BETA, GAMMA, ALPHA, FIRST = range(7)
    one = jnp.ones((8, LANES), F32)
    for v, t in ((CW, zero8), (AW, -one), (AX, zero8), (BETA, zero8), (GAMMA, one), (ALPHA, one)):
        k.cf[v] = t

    def scalars(step, gamma, delta):
        @pl.when(step == 1)
        def _():
            k.cf[ALPHA] = gamma / delta
            k.cf[FIRST] = gamma

        @pl.when(step > 1)
        def _():
            beta = gamma / k.cf[GAMMA]
            k.cf[BETA] = beta
            k.cf[ALPHA] = gamma / (delta - beta * gamma / k.cf[ALPHA])
            res[step - 2] = (gamma / k.cf[FIRST])[0, 0]
        k.cf[CW], k.cf[AW], k.cf[AX], k.cf[GAMMA] = one, k.cf[ALPHA], k.cf[ALPHA], gamma

    def phase(u, _):
        begin = u < 4
        n, ph = jnp.maximum(u - 4, 0) // 3, lax.rem(u + 2, 3)
        i = lax.rem(n, 2)
        step = n // 2
        b = lax.rem(step, 2)
        t = jnp.where(ph == 0, 0, jnp.where((ph == 1) == (i == 0), 1, 2))
        live = u >= 4
        more = n < 2 * ITERS - 1

        @pl.when(begin)
        def _():
            lax.fori_loop(ZL * u, ZL * (u + 1), load_step, 0)

        @pl.when(live & (i == 0) & (ph == 2) & (step > 0))
        def _():
            sum_next(b)

        @pl.when(live & (i == 1) & (ph == 0))
        def _():
            @pl.when(step > 0)
            def _():
                scalars(step, *sum_end(b, 2))
            k.gd[0], k.gd[1] = zero8, zero8

        @pl.when(live)
        def _():
            receive(i, t)

            @pl.when(i == 0)
            def _():
                finish(0, t, store_odd)

            @pl.when(i == 1)
            def _():
                finish(1, t, update_even)

        o = jnp.where(begin, 0, 1 - i)

        def send_one(g, _):
            send(o, g)
            return 0

        lax.fori_loop(jnp.where(begin, 0, t), jnp.where(begin, jnp.where(u == 0, 3, 0), jnp.where(more, t + 1, t)), send_one, 0)

        @pl.when((begin & (u > 0)) | (live & more))
        def _():
            tell(o, jnp.where(begin, u - 1, t))

        def post_one(e, _):
            late = begin | (e == 2)
            post(jnp.where(late, o, i), jnp.where(begin, u - 1, jnp.where(late, 0, e + 1)))
            return 0

        first = jnp.where(begin | (n == 0), 2, 0)
        busy = jnp.where(begin, u > 0, ph == 0)
        lax.fori_loop(first, jnp.where(busy, jnp.where(more, 3, 2), first), post_one, 0)

        @pl.when(live & (ph == 2))
        def _():
            for m in range(6):
                z_copy(i, m).wait_send()
            for g in range(3):
                for cp in h_copies(i, g):
                    cp.wait_send()

            @pl.when((i == 1) & more)
            def _():
                sum_start(1 - b, 2)
        return 0

    lax.fori_loop(0, 4 + 3 * 2 * ITERS, phase, 0)

    def dots(j, carry):
        for c in COMPS:
            w, r, s = k.f[j, c, pl.ds(R0, ROWS), :], k.r[j, c], k.s[j, c]
            carry = tuple(t + u * v for t, (u, v) in zip(carry, ((r, r), (w, r), (w, w), (r, s), (w, s), (s, s))))
        return carry

    for v, t in enumerate(lax.fori_loop(0, ZL, dots, (jnp.zeros((ROWS, LANES), F32),) * 6)):
        k.gd[v] = sum(t[8 * b:8 * b + 8] for b in range(4))
    sum_start(0, 6)
    sum_next(0)
    rr, wr, ww, rs, ws, ss = sum_end(0, 6)
    beta = rr / k.cf[GAMMA]
    alpha = rr / (wr - beta * rr / k.cf[ALPHA])
    last = rr - 2.0 * alpha * (wr + beta * rs) + alpha * alpha * (ww + 2.0 * beta * ws + beta * beta * ss)
    for v, t in ((ITERS - 2, rr), (ITERS - 1, last)):
        res[v] = (t / k.cf[FIRST])[0, 0]
    alpha, beta = (jnp.broadcast_to(v[0:1], (ROWS, LANES)) for v in (alpha, beta))

    def out_plane(j, _):
        for c in COMPS:
            v = k.x[j, c] + alpha * (k.r[j, c] + beta * k.p[j, c])
            for s in range(2):
                k.sst[pl.ds(j * SITE + 6 * s + c, VALID, 12), :] = rot(v, HALF * s)[0:VALID, 0:YL]
        return 0

    lax.fori_loop(0, ZL, out_plane, 0)
    each_src(lambda *a: out_copy(*a).start())
    each_src(lambda *a: out_copy(*a).wait())


def solution(mesh):
    link_spec = P(None, 't', 'zz', 'yy', None, None, None, None)
    field_spec = P('t', 'zz', 'yy', None, None, None)

    def local_solve(fat_links, long_links, source, quark_mass):
        fat, lng = (jnp.transpose(v, (0, 1, 2, 4, 5, 6, 7, 3)).reshape(4, TL, ZL, SITE, YL) for v in (fat_links, long_links))
        src = jnp.transpose(source, (0, 1, 3, 4, 5, 2)).reshape(TL, SITE, YL)
        anywhere, scalar = (pl.BlockSpec(memory_space=space) for space in (pl.ANY, pltpu.SMEM))
        sol, res = pl.pallas_call(
            kernel,
            out_shape=tuple(jax.ShapeDtypeStruct(shape, F32) for shape in ((TL, SITE, YL), (8,))),
            in_specs=[anywhere] * 3 + [scalar],
            out_specs=(anywhere, scalar),
            scratch_shapes=list(SCRATCH.values()),
            compiler_params=pltpu.CompilerParams(collective_id=0, has_side_effects=True, vmem_limit_bytes=67043328),
            name='cg',
        )(fat, lng, src, quark_mass)
        return jnp.transpose(sol.reshape(TL, ZL, XH, 3, 2, YL), (0, 1, 5, 2, 3, 4)), res

    return jax.shard_map(local_solve, mesh=mesh, in_specs=(link_spec, link_spec, field_spec, P(None)), out_specs=(field_spec, P()), check_vma=False)
```

time: 203 us -> 188 us (0.926)
  Pallas kernels: 198 us -> 184 us
    pallas_call x1, Pallas kernels: 198 us -> 184 us  [local_solve(): pl.pallas_call(kernel, out_shape=tuple((jax.ShapeDtypeStruct(shape, F32)...]
where the time goes in v2:
time: 188 us
  Pallas kernels  184 us (98%)
  local copies, waits for them, and re-layouts  3.13 us (2%)
    pallas_call x1, Pallas kernels, local_solve(): pl.pallas_call(kernel, out_shape=tuple((jax.ShapeDtypeStruct(shape, F32)...  184 us

profile of v2, /device:TPU:0, one launch (start us, length us, event | category | flops | bytes accessed | tf_op | source)
XLA Modules:
  0.0 188.0 jit_solution(12492569669082886222)
XLA Ops:
  1.3 183.5 %cg.1 = (f32[6,360,48]{2,1,0:T(8,128)}, f32[8]{0:T(128)}) custom-call(f32[4,6,6,360,48]{4,3,2,1,0:T(8,128)} %bitcast.12, f32[4,6,6,360,48]{4,3,2,1,0:T(8,128)} %bitcast.13, f32[6,360,48]{2,1,0:T(8,128)} %bitcast.14, f32[1]{0:T(128)S(6)} %copy.8.mass), custom_call_target="tpu_custom_call" | custom-call | tf_op jit(solution)/shard_map/cg/pallas_call | solution.py:600
  184.8 0.0 copy-start
  184.8 2.6 %copy.9 = f32[6,6,48,10,3,2]{2,5,4,3,1,0:T(2,128)} copy(f32[6,6,48,10,3,2]{2,5,4,3,1,0:T(2,128)} %bitcast.15) | data formatting | bytes 829440
  187.4 0.0 copy-done
  187.4 0.5 copy.10
Async XLA Ops:
  184.8 2.6 %copy-start = (f32[8]{0:T(128)S(1)}, f32[8]{0:T(128)}, u32[]{:S(2)}) copy-start(f32[8]{0:T(128)} %get-tuple-element.9) | copy-start | bytes 100

commit v3 on v2

--- a/solution.py
+++ b/solution.py
@@ -161,6 +161,7 @@
     k.lkt[:, :, 0:R0, :] = jnp.zeros((24, 18, R0, LANES), F32)
     k.lkt[:, :, R0 + ROWS:, :] = jnp.zeros((24, 18, 8, LANES), F32)
 
+    k.stg[:, SITE * TL:, :] = jnp.zeros((2 * NSTG, 144, YL), F32)
     z16 = jnp.zeros((ROWS, R0), F32)
 
     def both(half):
@@ -179,17 +180,18 @@
 
     def convert(g, zi, ref, base, lead):
         slot = lax.rem(g, NSTG)
-        even = (((row // XL + lane + zi) & 1) == 0)[:, 0:YL]
-
-        def some_comps(q, _):
-            for n in range(2):
-                for u in range(3):
-                    c = 3 * q + u
-                    v = [[k.stg[2 * slot + n, pl.ds(c + (2 * s + h) * 18, ROWS, 72), :] for h in range(2)] for s in range(2)]
-                    for o in range(2):
-                        ref[lead(n, o, zi), c, pl.ds(base, ROWS), :] = both([jnp.where(even, v[s][o], v[s][1 - o]) for s in range(2)])
-            return 0
-        lax.fori_loop(0, 6, some_comps, 0)
+        even = ((row // XL + lane + zi) & 1) == 0
+        rest = jnp.zeros((ROWS, LANES - YL), F32)
+
+        def whole(n, c, h):
+            v = [jnp.concatenate([k.stg[2 * slot + n, pl.ds(c + (2 * s + h) * 18, ROWS, 72), :], rest], axis=1) for s in range(2)]
+            return v[0] + rot(v[1], HALF)
+
+        for n in range(2):
+            for c in LINKS:
+                v = [whole(n, c, h) for h in range(2)]
+                for o in range(2):
+                    ref[lead(n, o, zi), c, pl.ds(base, ROWS), :] = jnp.where(even, v[o], v[1 - o])
 
     def load_step(g, _):
         di, zi = what(g)
@@ -211,7 +213,7 @@
         return 0
 
     def z_copy(i, m):
-        return remote(k.zs.at[i, m], k.zr.at[i, m], k.z_ss.at[i, m], k.z_rs.at[i, m], at_z())
+        return remote(k.zs.at[i, m, used], k.zr.at[i, m, used], k.z_ss.at[i, m], k.z_rs.at[i, m], at_z())
 
     def h_copies(i, t):
         pairs = ((k.tsf, k.trf, at_t(3)), (k.tsc, k.trc, at_t(1)), (k.ysf, k.yrf, at_y(3)), (k.ysc, k.yrc, at_y(1)))
@@ -219,6 +221,7 @@
         return [remote(a.at[i, two], b.at[i, two], k.h_ss.at[i, t, n], k.h_rs.at[i, t, n], dev) for n, (a, b, dev) in enumerate(pairs)]
 
     gap = ylane8 >= YL
+    used = pl.ds(0, 135)
 
     def rows_of(u, part, off=0):
         return pl.ds(off + 15 * (u % 2) + part, 8)
@@ -487,18 +490,21 @@
         k.cf[CW], k.cf[AW], k.cf[AX], k.cf[GAMMA] = one, k.cf[ALPHA], k.cf[ALPHA], gamma
 
     def phase(u, _):
-        begin = u < 4
-        n, ph = jnp.maximum(u - 4, 0) // 3, lax.rem(u + 2, 3)
+        last = u == 4
+        begin = (u < 3) | last
+        load = jnp.where(last, 3, u)
+        v = jnp.where(u == 3, 0, jnp.maximum(u - 4, 0))
+        n, ph = v // 3, lax.rem(v, 3)
         i = lax.rem(n, 2)
         step = n // 2
         b = lax.rem(step, 2)
         t = jnp.where(ph == 0, 0, jnp.where((ph == 1) == (i == 0), 1, 2))
-        live = u >= 4
+        live = jnp.logical_not(begin)
         more = n < 2 * ITERS - 1
 
         @pl.when(begin)
         def _():
-            lax.fori_loop(ZL * u, ZL * (u + 1), load_step, 0)
+            lax.fori_loop(ZL * load, ZL * (load + 1), load_step, 0)
 
         @pl.when(live & (i == 0) & (ph == 2) & (step > 0))
         def _():
@@ -533,11 +539,11 @@
 
         @pl.when((begin & (u > 0)) | (live & more))
         def _():
-            tell(o, jnp.where(begin, u - 1, t))
+            tell(o, jnp.where(begin, load - 1, t))
 
         def post_one(e, _):
             late = begin | (e == 2)
-            post(jnp.where(late, o, i), jnp.where(begin, u - 1, jnp.where(late, 0, e + 1)))
+            post(jnp.where(late, o, i), jnp.where(begin, load - 1, jnp.where(late, 0, e + 1)))
             return 0
 
         first = jnp.where(begin | (n == 0), 2, 0)
@@ -569,29 +575,38 @@
         k.gd[v] = sum(t[8 * b:8 * b + 8] for b in range(4))
     sum_start(0, 6)
     sum_next(0)
+    parts = (k.sst, k.stg.at[0], k.stg.at[1])
+
+    def out_plane(j, _):
+        for to, frm in zip(parts, (k.x, k.r, k.p)):
+            for c in COMPS:
+                for s in range(2):
+                    to[pl.ds(j * SITE + 6 * s + c, VALID, 12), :] = rot(frm[j, c], HALF * s)[0:VALID, 0:YL]
+        return 0
+
+    lax.fori_loop(0, ZL, out_plane, 0)
     rr, wr, ww, rs, ws, ss = sum_end(0, 6)
     beta = rr / k.cf[GAMMA]
     alpha = rr / (wr - beta * rr / k.cf[ALPHA])
     last = rr - 2.0 * alpha * (wr + beta * rs) + alpha * alpha * (ww + 2.0 * beta * ws + beta * beta * ss)
     for v, t in ((ITERS - 2, rr), (ITERS - 1, last)):
         res[v] = (t / k.cf[FIRST])[0, 0]
-    alpha, beta = (jnp.broadcast_to(v[0:1], (ROWS, LANES)) for v in (alpha, beta))
-
-    def out_plane(j, _):
-        for c in COMPS:
-            v = k.x[j, c] + alpha * (k.r[j, c] + beta * k.p[j, c])
-            for s in range(2):
-                k.sst[pl.ds(j * SITE + 6 * s + c, VALID, 12), :] = rot(v, HALF * s)[0:VALID, 0:YL]
+    alpha, beta = (jnp.broadcast_to(v[0:1, 0:YL], (SITE, YL)) for v in (alpha, beta))
+
+    def out_rows(j, _):
+        here = pl.ds(j * SITE, SITE)
+        x, r, p = (ref[here, :] for ref in parts)
+        k.sst[here, :] = x + alpha * (r + beta * p)
         return 0
 
-    lax.fori_loop(0, ZL, out_plane, 0)
+    lax.fori_loop(0, ZL, out_rows, 0)
     each_src(lambda *a: out_copy(*a).start())
     each_src(lambda *a: out_copy(*a).wait())
 
 
 def solution(mesh):
-    link_spec = P(None, 't', 'zz', 'yy', None, None, None, None)
-    field_spec = P('t', 'zz', 'yy', None, None, None)
+    link_spec = P(None, 't', 'zz', 'yy')
+    field_spec = P('t', 'zz', 'yy')
 
     def local_solve(fat_links, long_links, source, quark_mass):
         fat, lng = (jnp.transpose(v, (0, 1, 2, 4, 5, 6, 7, 3)).reshape(4, TL, ZL, SITE, YL) for v in (fat_links, long_links))
@@ -608,4 +623,4 @@
         )(fat, lng, src, quark_mass)
         return jnp.transpose(sol.reshape(TL, ZL, XH, 3, 2, YL), (0, 1, 5, 2, 3, 4)), res
 
-    return jax.shard_map(local_solve, mesh=mesh, in_specs=(link_spec, link_spec, field_spec, P(None)), out_specs=(field_spec, P()), check_vma=False)
+    return jax.shard_map(local_solve, mesh=mesh, in_specs=(link_spec, link_spec, field_spec, P()), out_specs=(field_spec, P()), check_vma=False)

time: 188 us -> 180 us (0.957)
  Pallas kernels: 184 us -> 176 us
    pallas_call x1, Pallas kernels: 184 us -> 176 us  [local_solve(): pl.pallas_call(kernel, out_shape=tuple((jax.ShapeDtypeStruct(shape, F32)...]
where the time goes in v3:
time: 180 us
  Pallas kernels  176 us (98%)
  local copies, waits for them, and re-layouts  3.13 us (2%)
    pallas_call x1, Pallas kernels, local_solve(): pl.pallas_call(kernel, out_shape=tuple((jax.ShapeDtypeStruct(shape, F32)...  176 us

profile of v3, /device:TPU:0, one launch (start us, length us, event | category | flops | bytes accessed | tf_op | source)
XLA Modules:
  0.0 180.1 jit_solution(6191341401878271219)
XLA Ops:
  1.3 175.7 %cg.1 = (f32[6,360,48]{2,1,0:T(8,128)}, f32[8]{0:T(128)}) custom-call(f32[4,6,6,360,48]{4,3,2,1,0:T(8,128)} %bitcast.12, f32[4,6,6,360,48]{4,3,2,1,0:T(8,128)} %bitcast.13, f32[6,360,48]{2,1,0:T(8,128)} %bitcast.14, f32[1]{0:T(128)S(6)} %copy.8.mass), custom_call_target="tpu_custom_call" | custom-call | tf_op jit(solution)/shard_map/cg/pallas_call | solution.py:615
  177.0 0.0 copy-start
  177.0 2.6 %copy.9 = f32[6,6,48,10,3,2]{2,5,4,3,1,0:T(2,128)} copy(f32[6,6,48,10,3,2]{2,5,4,3,1,0:T(2,128)} %bitcast.15) | data formatting | bytes 829440
  179.6 0.0 copy-done
  179.6 0.5 copy.10
Async XLA Ops:
  177.0 2.6 %copy-start = (f32[8]{0:T(128)S(1)}, f32[8]{0:T(128)}, u32[]{:S(2)}) copy-start(f32[8]{0:T(128)} %get-tuple-element.9) | copy-start | bytes 100

commit v4 on v3

--- a/solution.py
+++ b/solution.py
@@ -17,11 +17,36 @@
 C0 = 3
 STEPS = ((0, 1), (1, 3))
 SITE = VALID * 2 * 6
+ORDER = 'z3z4z5t1y1t4y4z0z1x1x4t0y0t2y2t3y3t5y5x0x2z2x3x5'
+FIRST_STEP = 'aadhlpptwwyy'
 LOADS = 4 * ZL
+PITCH, QUAD = 76, 72
 BLK = 16
 BLOCKS = range(0, ROWS, BLK)
 
 
+def packed(values):
+    return [sum(v << 5 * q for q, v in enumerate(values[w:w + 6])) for w in range(0, len(values), 6)]
+
+
+def pick(words, q):
+    word = words[-1]
+    for w, value in enumerate(words[:-1]):
+        word = jnp.where(q // 6 == w, value, word)
+    return (word >> 5 * lax.rem(q, 6)) & 31
+
+
+STEP_WORDS = packed(['tzyx'.index(ORDER[q]) * 8 + int(ORDER[q + 1]) for q in range(0, 2 * LOADS, 2)])
+PHASE_WORDS = packed([ord(q) - ord('a') for q in FIRST_STEP])
+
+
+def loop(first, last, act):
+    def body(q, carry):
+        act(q)
+        return carry
+    lax.fori_loop(first, last, body, 0)
+
+
 def vec(*shape):
     return pltpu.VMEM(shape + (LANES,), F32)
 
@@ -43,32 +68,35 @@
 
 
 SCRATCH = dict(
-    lkt=vec(24, 18, 56), lko=vec(72, 18, ROWS), stg=pltpu.VMEM((2 * NSTG, 2304, YL), F32), sst=pltpu.VMEM((2304, YL), F32),
+    lkt=vec(24, 18, 56), lko=vec(72, 18, ROWS), stg=pltpu.VMEM((2 * NSTG, ROWS * PITCH, YL), F32), sst=pltpu.VMEM((2304, YL), F32),
     f=vec(18, 6, 64), acc=plane(), cb=vec(2, 6, ROWS), xs=vec(2, 6, YL),
     r=plane(), p=plane(), s=plane(), z=plane(), x=plane(), zs=vec(2, 6, 136), zr=vec(2, 6, 136),
     tsf=halo_t(), trf=halo_t(), tsc=halo_t(), trc=halo_t(), ysf=halo_y(), yrf=halo_y(), ysc=halo_y(), yrc=halo_y(),
-    ra=vec(2, 8, 8), rb=vec(2, 4, 8), gd=vec(6, 8), cf=vec(8, 8),
-    stg_sem=sems(NSTG, 12), io_sem=sems(36), z_ss=sems(2, 6), z_rs=sems(2, 6), h_ss=sems(2, 3, 4), h_rs=sems(2, 3, 4),
-    a_ss=sems(2, 10), a_rs=sems(2, 10),
+    ra=vec(2, 32), gd=vec(6, 8), cf=vec(8, 8),
+    stg_sem=sems(NSTG, 2), io_sem=sems(ZL), m_sem=sems(1), ms=pltpu.VMEM((1, 1), F32), z_ss=sems(2), z_rs=sems(2, 6), h_ss=sems(2, 4), h_rs=sems(2, 3, 4),
+    a_ss=sems(2), a_rs=sems(2),
 )
 
 
-def mat(acc, link, psi):
+def terms(link, psi):
     for i in range(3):
         for j in range(3):
-            a, b = link(6 * i + 2 * j), link(6 * i + 2 * j + 1)
-            c, d = psi[2 * j], psi[2 * j + 1]
-            acc[2 * i] = acc[2 * i] + (a * c - b * d)
-            acc[2 * i + 1] = acc[2 * i + 1] + (a * d + b * c)
+            at = 2 * (3 * i + j)
+            yield i, j, link(at), link(at + 1), psi
+
+
+def mat(acc, link, psi):
+    for i, j, a, b, v in terms(link, psi):
+        c, d = v[2 * j:2 * j + 2]
+        acc[2 * i] = acc[2 * i] + (a * c - b * d)
+        acc[2 * i + 1] = acc[2 * i + 1] + (a * d + b * c)
 
 
 def adj(acc, link, psi):
-    for j in range(3):
-        for i in range(3):
-            a, b = link(6 * j + 2 * i), link(6 * j + 2 * i + 1)
-            c, d = psi[2 * j], psi[2 * j + 1]
-            acc[2 * i] = acc[2 * i] - (a * c + b * d)
-            acc[2 * i + 1] = acc[2 * i + 1] + (b * c - a * d)
+    for j, i, a, b, v in terms(link, psi):
+        c, d = v[2 * j:2 * j + 2]
+        acc[2 * i] = acc[2 * i] - (a * c + b * d)
+        acc[2 * i + 1] = acc[2 * i + 1] + (b * c - a * d)
 
 
 def rot(v, n):
@@ -85,8 +113,8 @@
     def at_t(d):
         return (iy, iz, lax.rem(it + d, 4))
 
-    def at_z(d=0):
-        return (iy, 1 - iz, lax.rem(it + d, 4))
+    def at_z():
+        return (iy, 1 - iz, it)
 
     def at_y(d):
         return (lax.rem(iy + d, 4), iz, it)
@@ -94,45 +122,41 @@
     def remote(src_ref, dst_ref, send, recv, dev):
         return pltpu.make_async_remote_copy(src_ref=src_ref, dst_ref=dst_ref, send_sem=send, recv_sem=recv, device_id=dev, device_id_type=MESH)
 
-    others = range(1, 4)
-    near = [at_t(d) for d in others] + [at_z(d) for d in range(4)]
-    ring = [at_y(d) for d in others]
+    def at_any(d):
+        return (iy + d // 8) & 3, (iz + d // 4) & 1, (it + d) & 3
+
+    def each_other(act):
+        for d in range(1, 32):
+            act(d)
 
     def plane_of(t, n2):
         first = jnp.where(t == 0, 1, jnp.where(t == 1, 0, 3))
         return first + n2 * jnp.where(t == 0, 3, 2)
 
     def what(g):
-        q = jnp.maximum(g - ZL, 0)
-        d = lax.rem(q, 3)
-        p = q // 3
-        early = g < ZL
-        return jnp.where(early, 1, jnp.where(d == 0, 0, d + 1)), jnp.where(early, g, plane_of(p // 2, lax.rem(p, 2)))
+        code = pick(STEP_WORDS, g)
+        return code // 8, code & 7
 
     def stg_copies(g):
         slot = lax.rem(g, NSTG)
         di, zi = what(g)
-        return [pltpu.make_async_copy(ref.at[di, t, zi], k.stg.at[2 * slot + n, pl.ds(SITE * t, SITE)], k.stg_sem.at[slot, TL * n + t])
-                for n, ref in enumerate((fat, lng)) for t in range(TL)]
-
-    def each_src(act):
-        for q in range(TL * ZL):
-            zi, ti = q // TL, q % TL
-            act(q, pl.ds(zi * SITE + ti * 60, 60), ti, pl.ds(zi * 60, 60))
-
-    def src_copy(q, here, ti, there):
-        return pltpu.make_async_copy(src.at[ti, there], k.sst.at[here], k.io_sem.at[q])
-
-    def out_copy(q, here, ti, there):
-        return pltpu.make_async_copy(k.sst.at[here], out.at[ti, there], k.io_sem.at[q])
-
-    barrier = pltpu.get_barrier_semaphore()
-    for dev in near + ring:
-        pl.semaphore_signal(barrier, inc=1, device_id=dev, device_id_type=MESH)
-    each_src(lambda *a: src_copy(*a).start())
+
+        def to(n):
+            return k.stg.at[2 * slot + n, pl.ds(0, VALID * PITCH)].reshape(TL, XL, PITCH, YL).at[:, :, pl.ds(0, QUAD)]
+        return [pltpu.make_async_copy(ref.at[di, :, zi], to(n), k.stg_sem.at[slot, n]) for n, ref in enumerate((fat, lng))]
+
+    def src_copy(zi):
+        return pltpu.make_async_copy(src.at[:, pl.ds(60 * zi, 60)], k.sst.at[pl.ds(SITE * zi, SITE)].reshape(TL, 60, YL), k.io_sem.at[zi])
+
+    mass_copy = pltpu.make_async_copy(mass, k.ms, k.m_sem.at[0])
+    mass_copy.start()
+    for zi in range(ZL):
+        src_copy(zi).start()
     for g in range(NSTG):
         for cp in stg_copies(jnp.int32(g)):
             cp.start()
+    barrier = pltpu.get_barrier_semaphore()
+    each_other(lambda d: pl.semaphore_signal(barrier, inc=1, device_id=at_any(d), device_id_type=MESH))
 
     lane8, row8 = (lax.broadcasted_iota(jnp.int32, (8, LANES), d) for d in (1, 0))
     ylane8 = lane8 % HALF
@@ -161,22 +185,17 @@
     k.lkt[:, :, 0:R0, :] = jnp.zeros((24, 18, R0, LANES), F32)
     k.lkt[:, :, R0 + ROWS:, :] = jnp.zeros((24, 18, 8, LANES), F32)
 
-    k.stg[:, SITE * TL:, :] = jnp.zeros((2 * NSTG, 144, YL), F32)
+    k.stg[:, VALID * PITCH:, :] = jnp.zeros((2 * NSTG, 2 * PITCH, YL), F32)
     z16 = jnp.zeros((ROWS, R0), F32)
 
     def both(half):
         return jnp.where(row < VALID, jnp.concatenate([half[0], z16, half[1], z16], axis=1), 0.0)
 
-    def src_plane(zi, _):
+    def src_plane(zi):
         for c in COMPS:
             v = both([k.sst[pl.ds(zi * SITE + 6 * s + c, ROWS, 12), :] for s in range(2)])
             k.f[zi, c, pl.ds(R0, ROWS), :] = v
             k.r[zi, c] = v
-        return 0
-
-    each_src(lambda *a: src_copy(*a).wait())
-    lax.fori_loop(0, ZL, src_plane, 0)
-    pl.semaphore_wait(barrier, len(near + ring))
 
     def convert(g, zi, ref, base, lead):
         slot = lax.rem(g, NSTG)
@@ -184,7 +203,7 @@
         rest = jnp.zeros((ROWS, LANES - YL), F32)
 
         def whole(n, c, h):
-            v = [jnp.concatenate([k.stg[2 * slot + n, pl.ds(c + (2 * s + h) * 18, ROWS, 72), :], rest], axis=1) for s in range(2)]
+            v = [jnp.concatenate([k.stg[2 * slot + n, pl.ds(c + (2 * s + h) * 18, ROWS, PITCH), :], rest], axis=1) for s in range(2)]
             return v[0] + rot(v[1], HALF)
 
         for n in range(2):
@@ -193,7 +212,7 @@
                 for o in range(2):
                     ref[lead(n, o, zi), c, pl.ds(base, ROWS), :] = jnp.where(even, v[o], v[1 - o])
 
-    def load_step(g, _):
+    def load_step(g):
         di, zi = what(g)
         for cp in stg_copies(g):
             cp.wait()
@@ -210,15 +229,19 @@
         def _():
             for cp in stg_copies(g + NSTG):
                 cp.start()
-        return 0
 
     def z_copy(i, m):
-        return remote(k.zs.at[i, m, used], k.zr.at[i, m, used], k.z_ss.at[i, m], k.z_rs.at[i, m], at_z())
-
-    def h_copies(i, t):
+        return remote(k.zs.at[i, m, used], k.zr.at[i, m, used], k.z_ss.at[i], k.z_rs.at[i, m], at_z())
+
+    def h_copies(i, t, whole=False):
         pairs = ((k.tsf, k.trf, at_t(3)), (k.tsc, k.trc, at_t(1)), (k.ysf, k.yrf, at_y(3)), (k.ysc, k.yrc, at_y(1)))
-        two = pl.ds(2 * t, 2)
-        return [remote(a.at[i, two], b.at[i, two], k.h_ss.at[i, t, n], k.h_rs.at[i, t, n], dev) for n, (a, b, dev) in enumerate(pairs)]
+        some = pl.ds(0, ZL) if whole else pl.ds(2 * t, 2)
+        return [remote(a.at[i, some], b.at[i, some], k.h_ss.at[i, n], k.h_rs.at[i, t, n], dev) for n, (a, b, dev) in enumerate(pairs)]
+
+    def sent(i):
+        remote(k.zs.at[i, :, used], k.zr.at[i, :, used], k.z_ss.at[i], k.z_rs.at[i, 0], at_z()).wait_send()
+        for cp in h_copies(i, 0, True):
+            cp.wait_send()
 
     gap = ylane8 >= YL
     used = pl.ds(0, 135)
@@ -316,7 +339,7 @@
             unpack_psi(i, 2)
 
     def tell(i, t):
-        def one_plane(n2, _):
+        def one_plane(n2):
             j = plane_of(t, n2)
             slot = 2 * t + n2
             fwd, bwd = zeros, zeros
@@ -343,16 +366,15 @@
                 for c in COMPS:
                     k.tsc[i, slot, c, pl.ds(8 * h, 8), :] = acc[c]
                     k.tsf[i, slot, c, pl.ds(8 * h, 8), :] = k.f[9 * i + j, c, pl.ds(R0 + 8 * h, 8), :]
-            return 0
-
-        lax.fori_loop(0, 2, one_plane, 0)
+
+        loop(0, 2, one_plane)
         for cp in h_copies(i, t):
             cp.start()
 
     def post(i, t):
         o = 1 - i
 
-        def one_plane(n2, _):
+        def one_plane(n2):
             j = plane_of(t, n2)
             for h in BLOCKS:
                 psi = psi_of(i, j, h)
@@ -381,11 +403,11 @@
                 mat(acc, lambda c: k.lko[lo(3, 1, o, j), c, at(h), :], [jnp.where(e, far[c], close[c]) for c in COMPS])
                 for c in COMPS:
                     k.acc[j, c, at(h), :] = acc[c]
-            return 0
-
-        lax.fori_loop(0, 2, one_plane, 0)
-
-    m2 = mass[0] * mass[0]
+
+        loop(0, 2, one_plane)
+
+    mass_copy.wait()
+    m2 = k.ms[0, 0] * k.ms[0, 0]
 
     def store_odd(j, h, real, acc):
         for c in COMPS:
@@ -416,7 +438,7 @@
         for cp in h_copies(i, t):
             cp.wait_recv()
 
-        def one_plane(n2, _):
+        def one_plane(n2):
             j = plane_of(t, n2)
             slot = 2 * t + n2
             for c in COMPS:
@@ -440,35 +462,27 @@
                 real = row_b + h < VALID
                 good = real & (ylane < YL)
                 update(j, h, real, [jnp.where(good, acc[c], 0.0) for c in COMPS])
-            return 0
-
-        lax.fori_loop(0, 2, one_plane, 0)
-
-    def a_copies(stage, b):
-        mine = k.rb.at[b, iy] if stage else k.ra.at[b, 4 * iz + it]
-        return [remote(mine, mine, k.a_ss.at[b, d], k.a_rs.at[b, d], dev) for d, dev in enumerate(near + ring) if (d >= len(near)) == bool(stage)]
+
+        loop(0, 2, one_plane)
+
+    me = 8 * iy + 4 * iz + it
+
+    def a_copy(b, first, rows, dev):
+        here = k.ra.at[b, pl.ds(first, rows)]
+        return remote(here, here, k.a_ss.at[b], k.a_rs.at[b], dev)
 
     def sum_start(b, n):
-        tile = zero8
+        mine = zeros[:1]
         for v in range(n):
-            tile = jnp.where(row8 == v, jnp.sum(k.gd[v], axis=0, keepdims=True), tile)
-        k.ra[b, 4 * iz + it] = tile
-        for cp in a_copies(0, b):
-            cp.start()
-
-    def sum_next(b):
-        for cp in a_copies(0, b):
-            cp.wait()
-        k.rb[b, iy] = sum(k.ra[b, d] for d in range(1, 8)) + k.ra[b, 0]
-        for cp in a_copies(1, b):
-            cp.start()
+            total = jnp.sum(jnp.sum(k.gd[v], axis=0, keepdims=True), axis=1, keepdims=True)
+            mine = jnp.where(lane[:1] == v, total, mine)
+        k.ra[b, pl.ds(me, 1), :] = mine
+        each_other(lambda d: a_copy(b, me, 1, at_any(d)).start())
 
     def sum_end(b, n):
-        for cp in a_copies(1, b):
-            cp.wait()
-        tile = sum(k.rb[b, d] for d in others) + k.rb[b, 0]
-        tile = jnp.broadcast_to(jnp.sum(tile, axis=1, keepdims=True), (8, LANES))
-        return [jnp.broadcast_to(tile[v:v + 1], (8, LANES)) for v in range(n)]
+        a_copy(b, 0, 31, at_z()).wait()
+        tile = jnp.sum(k.ra[b], axis=0, keepdims=True)
+        return [jnp.broadcast_to(tile[:, v:v + 1], (8, LANES)) for v in range(n)]
 
     CW, AW, AX, BETA, GAMMA, ALPHA, FIRST = range(7)
     one = jnp.ones((8, LANES), F32)
@@ -489,11 +503,9 @@
             res[step - 2] = (gamma / k.cf[FIRST])[0, 0]
         k.cf[CW], k.cf[AW], k.cf[AX], k.cf[GAMMA] = one, k.cf[ALPHA], k.cf[ALPHA], gamma
 
-    def phase(u, _):
-        last = u == 4
-        begin = (u < 3) | last
-        load = jnp.where(last, 3, u)
-        v = jnp.where(u == 3, 0, jnp.maximum(u - 4, 0))
+    def phase(u):
+        begin = (u < 5) | (u == 6) | (u == 7) | (u == 9)
+        v = jnp.where(u > 9, u - 8, jnp.where(u > 6, 1, 0))
         n, ph = v // 3, lax.rem(v, 3)
         i = lax.rem(n, 2)
         step = n // 2
@@ -504,11 +516,14 @@
 
         @pl.when(begin)
         def _():
-            lax.fori_loop(ZL * load, ZL * (load + 1), load_step, 0)
-
-        @pl.when(live & (i == 0) & (ph == 2) & (step > 0))
-        def _():
-            sum_next(b)
+            loop(pick(PHASE_WORDS, jnp.minimum(u, 10)), pick(PHASE_WORDS, jnp.minimum(u + 1, 10)), load_step)
+
+        @pl.when(u == 0)
+        def _():
+            for zi in range(ZL):
+                src_copy(zi).wait()
+            loop(0, ZL, src_plane)
+            pl.semaphore_wait(barrier, 31)
 
         @pl.when(live & (i == 1) & (ph == 0))
         def _():
@@ -529,41 +544,31 @@
             def _():
                 finish(1, t, update_even)
 
+        @pl.when(live & (ph == 2) & (i == 1) & more)
+        def _():
+            sum_start(1 - b, 2)
+
         o = jnp.where(begin, 0, 1 - i)
 
-        def send_one(g, _):
-            send(o, g)
-            return 0
-
-        lax.fori_loop(jnp.where(begin, 0, t), jnp.where(begin, jnp.where(u == 0, 3, 0), jnp.where(more, t + 1, t)), send_one, 0)
-
-        @pl.when((begin & (u > 0)) | (live & more))
-        def _():
-            tell(o, jnp.where(begin, load - 1, t))
-
-        def post_one(e, _):
+        loop(0, jnp.where(begin, jnp.where(u < 2, u + 1, 0), jnp.where(more, 1, 0)), lambda e: send(o, jnp.where(begin, jnp.where(u == 0, 1, 2 * e), t)))
+
+        @pl.when((begin & ((u == 2) | (u == 4) | (u == 6))) | (live & more))
+        def _():
+            tell(o, jnp.where(begin, u // 2 - 1, t))
+
+        def post_one(e):
             late = begin | (e == 2)
-            post(jnp.where(late, o, i), jnp.where(begin, load - 1, jnp.where(late, 0, e + 1)))
-            return 0
+            post(jnp.where(late, o, i), jnp.where(begin, u // 3 - 1, jnp.where(late, 0, e + 1)))
 
         first = jnp.where(begin | (n == 0), 2, 0)
-        busy = jnp.where(begin, u > 0, ph == 0)
-        lax.fori_loop(first, jnp.where(busy, jnp.where(more, 3, 2), first), post_one, 0)
+        busy = jnp.where(begin, (u == 3) | (u == 7) | (u == 9), ph == 0)
+        loop(first, jnp.where(busy, jnp.where(more, 3, 2), first), post_one)
 
         @pl.when(live & (ph == 2))
         def _():
-            for m in range(6):
-                z_copy(i, m).wait_send()
-            for g in range(3):
-                for cp in h_copies(i, g):
-                    cp.wait_send()
-
-            @pl.when((i == 1) & more)
-            def _():
-                sum_start(1 - b, 2)
-        return 0
-
-    lax.fori_loop(0, 4 + 3 * 2 * ITERS, phase, 0)
+            sent(i)
+
+    loop(0, 8 + 3 * 2 * ITERS, phase)
 
     def dots(j, carry):
         for c in COMPS:
@@ -574,17 +579,15 @@
     for v, t in enumerate(lax.fori_loop(0, ZL, dots, (jnp.zeros((ROWS, LANES), F32),) * 6)):
         k.gd[v] = sum(t[8 * b:8 * b + 8] for b in range(4))
     sum_start(0, 6)
-    sum_next(0)
     parts = (k.sst, k.stg.at[0], k.stg.at[1])
 
-    def out_plane(j, _):
+    def out_plane(j):
         for to, frm in zip(parts, (k.x, k.r, k.p)):
             for c in COMPS:
                 for s in range(2):
                     to[pl.ds(j * SITE + 6 * s + c, VALID, 12), :] = rot(frm[j, c], HALF * s)[0:VALID, 0:YL]
-        return 0
-
-    lax.fori_loop(0, ZL, out_plane, 0)
+
+    loop(0, ZL, out_plane)
     rr, wr, ww, rs, ws, ss = sum_end(0, 6)
     beta = rr / k.cf[GAMMA]
     alpha = rr / (wr - beta * rr / k.cf[ALPHA])
@@ -593,15 +596,14 @@
         res[v] = (t / k.cf[FIRST])[0, 0]
     alpha, beta = (jnp.broadcast_to(v[0:1, 0:YL], (SITE, YL)) for v in (alpha, beta))
 
-    def out_rows(j, _):
+    def out_rows(j):
         here = pl.ds(j * SITE, SITE)
         x, r, p = (ref[here, :] for ref in parts)
-        k.sst[here, :] = x + alpha * (r + beta * p)
-        return 0
-
-    lax.fori_loop(0, ZL, out_rows, 0)
-    each_src(lambda *a: out_copy(*a).start())
-    each_src(lambda *a: out_copy(*a).wait())
+        v = x + alpha * (r + beta * p)
+        for t in range(TL):
+            out[t, pl.ds(j * 60, 60), :] = v[60 * t:60 * (t + 1)]
+
+    loop(0, ZL, out_rows)
 
 
 def solution(mesh):
@@ -609,18 +611,18 @@
     field_spec = P('t', 'zz', 'yy')
 
     def local_solve(fat_links, long_links, source, quark_mass):
-        fat, lng = (jnp.transpose(v, (0, 1, 2, 4, 5, 6, 7, 3)).reshape(4, TL, ZL, SITE, YL) for v in (fat_links, long_links))
+        fat, lng = (jnp.transpose(v, (0, 1, 2, 4, 5, 6, 7, 3)).reshape(4, TL, ZL, XL, QUAD, YL) for v in (fat_links, long_links))
         src = jnp.transpose(source, (0, 1, 3, 4, 5, 2)).reshape(TL, SITE, YL)
-        anywhere, scalar = (pl.BlockSpec(memory_space=space) for space in (pl.ANY, pltpu.SMEM))
+        anywhere, local, scalar = (pl.BlockSpec(memory_space=space) for space in (pl.ANY, pltpu.VMEM, pltpu.SMEM))
         sol, res = pl.pallas_call(
             kernel,
-            out_shape=tuple(jax.ShapeDtypeStruct(shape, F32) for shape in ((TL, SITE, YL), (8,))),
-            in_specs=[anywhere] * 3 + [scalar],
-            out_specs=(anywhere, scalar),
+            out_shape=(pltpu.VMEM((TL, SITE, YL), F32), pltpu.SMEM((8,), F32)),
+            in_specs=[anywhere] * 4,
+            out_specs=(local, scalar),
             scratch_shapes=list(SCRATCH.values()),
-            compiler_params=pltpu.CompilerParams(collective_id=0, has_side_effects=True, vmem_limit_bytes=67043328),
+            compiler_params=pltpu.CompilerParams(collective_id=0, has_side_effects=True, vmem_limit_bytes=60000000),
             name='cg',
-        )(fat, lng, src, quark_mass)
+        )(fat, lng, src, quark_mass.reshape(1, 1))
         return jnp.transpose(sol.reshape(TL, ZL, XH, 3, 2, YL), (0, 1, 5, 2, 3, 4)), res
 
     return jax.shard_map(local_solve, mesh=mesh, in_specs=(link_spec, link_spec, field_spec, P()), out_specs=(field_spec, P()), check_vma=False)

time: 180 us -> 170 us (0.944)
  Pallas kernels: 176 us -> 167 us
    pallas_call x1, Pallas kernels: 176 us -> 167 us  [local_solve(): pl.pallas_call(kernel, out_shape=(pltpu.VMEM((TL, SITE, YL), F32), pltpu....]
where the time goes in v4:
time: 170 us
  Pallas kernels  167 us (98%)
    pallas_call x1, Pallas kernels, local_solve(): pl.pallas_call(kernel, out_shape=(pltpu.VMEM((TL, SITE, YL), F32), pltpu....  167 us

profile of v4, /device:TPU:0, one launch (start us, length us, event | category | flops | bytes accessed | tf_op | source)
XLA Modules:
  0.0 169.9 jit_solution(13200110420308486373)
XLA Ops:
  1.3 167.1 %cg.1 = (f32[6,360,48]{2,1,0:T(8,128)S(1)}, f32[8]{0:T(128)S(4)}) custom-call(f32[4,6,6,5,72,48]{5,4,3,2,1,0:T(8,128)} %bitcast.15, f32[4,6,6,5,72,48]{5,4,3,2,1,0:T(8,128)} %bitcast.16, f32[6,360,48]{2,1,0:T(8,128)} %bitcast.17, f32[1,1]{1,0:T(1,128)} %bitcast.13.mass), custom_call_target="tpu_custom_call" | custom-call | tf_op jit(solution)/shard_map/cg/pallas_call | solution.py:617
  168.4 1.0 copy.8
  169.4 0.5 copy.9

commit v5 on v4

--- a/solution.py
+++ b/solution.py
@@ -12,7 +12,7 @@
 R0 = 16
 ROWS, LANES, HALF, VALID = 32, 128, 64, 30
 XL = 5
-NSTG = 4
+NSTG = 6
 COMPS, LINKS = range(6), range(18)
 C0 = 3
 STEPS = ((0, 1), (1, 3))
@@ -63,6 +63,10 @@
     return vec(2, ZL, 6, R0)
 
 
+def wires():
+    return vec(2, 6, 136)
+
+
 def halo_y():
     return vec(2, ZL, BLK)
 
@@ -70,11 +74,11 @@
 SCRATCH = dict(
     lkt=vec(24, 18, 56), lko=vec(72, 18, ROWS), stg=pltpu.VMEM((2 * NSTG, ROWS * PITCH, YL), F32), sst=pltpu.VMEM((2304, YL), F32),
     f=vec(18, 6, 64), acc=plane(), cb=vec(2, 6, ROWS), xs=vec(2, 6, YL),
-    r=plane(), p=plane(), s=plane(), z=plane(), x=plane(), zs=vec(2, 6, 136), zr=vec(2, 6, 136),
+    r=plane(), p=plane(), s=plane(), z=plane(), x=plane(), zs=wires(), zr=wires(),
     tsf=halo_t(), trf=halo_t(), tsc=halo_t(), trc=halo_t(), ysf=halo_y(), yrf=halo_y(), ysc=halo_y(), yrc=halo_y(),
     ra=vec(2, 32), gd=vec(6, 8), cf=vec(8, 8),
-    stg_sem=sems(NSTG, 2), io_sem=sems(ZL), m_sem=sems(1), ms=pltpu.VMEM((1, 1), F32), z_ss=sems(2), z_rs=sems(2, 6), h_ss=sems(2, 4), h_rs=sems(2, 3, 4),
-    a_ss=sems(2), a_rs=sems(2),
+    stg_sem=sems(NSTG, 2), io_sem=sems(ZL), z_ss=sems(2), z_rs=sems(2, 6), h_ss=sems(2, 4), h_rs=sems(2, 3, 4),
+    a_ss=sems(2, 2), a_rs=sems(2, 2),
 )
 
 
@@ -122,12 +126,7 @@
     def remote(src_ref, dst_ref, send, recv, dev):
         return pltpu.make_async_remote_copy(src_ref=src_ref, dst_ref=dst_ref, send_sem=send, recv_sem=recv, device_id=dev, device_id_type=MESH)
 
-    def at_any(d):
-        return (iy + d // 8) & 3, (iz + d // 4) & 1, (it + d) & 3
-
-    def each_other(act):
-        for d in range(1, 32):
-            act(d)
+    slab = [((iy + d // 4) & 3, iz, (it + d) & 3) for d in range(1, R0)]
 
     def plane_of(t, n2):
         first = jnp.where(t == 0, 1, jnp.where(t == 1, 0, 3))
@@ -148,15 +147,14 @@
     def src_copy(zi):
         return pltpu.make_async_copy(src.at[:, pl.ds(60 * zi, 60)], k.sst.at[pl.ds(SITE * zi, SITE)].reshape(TL, 60, YL), k.io_sem.at[zi])
 
-    mass_copy = pltpu.make_async_copy(mass, k.ms, k.m_sem.at[0])
-    mass_copy.start()
     for zi in range(ZL):
         src_copy(zi).start()
     for g in range(NSTG):
         for cp in stg_copies(jnp.int32(g)):
             cp.start()
     barrier = pltpu.get_barrier_semaphore()
-    each_other(lambda d: pl.semaphore_signal(barrier, inc=1, device_id=at_any(d), device_id_type=MESH))
+    for dev in slab + [at_z()]:
+        pl.semaphore_signal(barrier, inc=1, device_id=dev, device_id_type=MESH)
 
     lane8, row8 = (lax.broadcasted_iota(jnp.int32, (8, LANES), d) for d in (1, 0))
     ylane8 = lane8 % HALF
@@ -186,29 +184,23 @@
     k.lkt[:, :, R0 + ROWS:, :] = jnp.zeros((24, 18, 8, LANES), F32)
 
     k.stg[:, VALID * PITCH:, :] = jnp.zeros((2 * NSTG, 2 * PITCH, YL), F32)
-    z16 = jnp.zeros((ROWS, R0), F32)
-
-    def both(half):
-        return jnp.where(row < VALID, jnp.concatenate([half[0], z16, half[1], z16], axis=1), 0.0)
+    def whole(half):
+        rest = jnp.zeros((ROWS, LANES - YL), F32)
+        first, second = (jnp.concatenate([v, rest], axis=1) for v in half)
+        return first + rot(second, HALF)
 
     def src_plane(zi):
         for c in COMPS:
-            v = both([k.sst[pl.ds(zi * SITE + 6 * s + c, ROWS, 12), :] for s in range(2)])
+            v = jnp.where(row < VALID, whole([k.sst[pl.ds(zi * SITE + 6 * s + c, ROWS, 12), :] for s in range(2)]), 0.0)
             k.f[zi, c, pl.ds(R0, ROWS), :] = v
             k.r[zi, c] = v
 
     def convert(g, zi, ref, base, lead):
         slot = lax.rem(g, NSTG)
         even = ((row // XL + lane + zi) & 1) == 0
-        rest = jnp.zeros((ROWS, LANES - YL), F32)
-
-        def whole(n, c, h):
-            v = [jnp.concatenate([k.stg[2 * slot + n, pl.ds(c + (2 * s + h) * 18, ROWS, PITCH), :], rest], axis=1) for s in range(2)]
-            return v[0] + rot(v[1], HALF)
-
         for n in range(2):
             for c in LINKS:
-                v = [whole(n, c, h) for h in range(2)]
+                v = [whole([k.stg[2 * slot + n, pl.ds(c + (2 * s + h) * 18, ROWS, PITCH), :] for s in range(2)]) for h in range(2)]
                 for o in range(2):
                     ref[lead(n, o, zi), c, pl.ds(base, ROWS), :] = jnp.where(even, v[o], v[1 - o])
 
@@ -406,8 +398,7 @@
 
         loop(0, 2, one_plane)
 
-    mass_copy.wait()
-    m2 = k.ms[0, 0] * k.ms[0, 0]
+    m2 = mass[0] * mass[0]
 
     def store_odd(j, h, real, acc):
         for c in COMPS:
@@ -465,23 +456,29 @@
 
         loop(0, 2, one_plane)
 
-    me = 8 * iy + 4 * iz + it
-
-    def a_copy(b, first, rows, dev):
+    me = R0 + 4 * iy + it
+
+    def a_copy(b, stage, first, rows, dev):
         here = k.ra.at[b, pl.ds(first, rows)]
-        return remote(here, here, k.a_ss.at[b], k.a_rs.at[b], dev)
+        return remote(here, here, k.a_ss.at[b, stage], k.a_rs.at[b, stage], dev)
 
     def sum_start(b, n):
         mine = zeros[:1]
         for v in range(n):
             total = jnp.sum(jnp.sum(k.gd[v], axis=0, keepdims=True), axis=1, keepdims=True)
             mine = jnp.where(lane[:1] == v, total, mine)
-        k.ra[b, pl.ds(me, 1), :] = mine
-        each_other(lambda d: a_copy(b, me, 1, at_any(d)).start())
+        k.ra[b, pl.ds(iz, 1), :] = mine
+        a_copy(b, 0, iz, 1, at_z()).start()
+
+    def sum_next(b):
+        a_copy(b, 0, 0, 1, at_z()).wait()
+        k.ra[b, pl.ds(me, 1), :] = k.ra[b, 0:1, :] + k.ra[b, 1:2, :]
+        for dev in slab:
+            a_copy(b, 1, me, 1, dev).start()
 
     def sum_end(b, n):
-        a_copy(b, 0, 31, at_z()).wait()
-        tile = jnp.sum(k.ra[b], axis=0, keepdims=True)
+        a_copy(b, 1, R0, len(slab), at_z()).wait()
+        tile = jnp.sum(k.ra[b, R0:], axis=0, keepdims=True)
         return [jnp.broadcast_to(tile[:, v:v + 1], (8, LANES)) for v in range(n)]
 
     CW, AW, AX, BETA, GAMMA, ALPHA, FIRST = range(7)
@@ -523,7 +520,11 @@
             for zi in range(ZL):
                 src_copy(zi).wait()
             loop(0, ZL, src_plane)
-            pl.semaphore_wait(barrier, 31)
+            pl.semaphore_wait(barrier, R0)
+
+        @pl.when(live & (i == 0) & (ph == 1) & (step > 0))
+        def _():
+            sum_next(b)
 
         @pl.when(live & (i == 1) & (ph == 0))
         def _():
@@ -560,9 +561,9 @@
             late = begin | (e == 2)
             post(jnp.where(late, o, i), jnp.where(begin, u // 3 - 1, jnp.where(late, 0, e + 1)))
 
-        first = jnp.where(begin | (n == 0), 2, 0)
-        busy = jnp.where(begin, (u == 3) | (u == 7) | (u == 9), ph == 0)
-        loop(first, jnp.where(busy, jnp.where(more, 3, 2), first), post_one)
+        own = live & (ph == 0) & (n > 0)
+        next_one = jnp.where(begin, (u == 3) | (u == 7) | (u == 9), (ph == 2) & more)
+        loop(jnp.where(own, 0, 2), jnp.where(next_one, 3, 2), post_one)
 
         @pl.when(live & (ph == 2))
         def _():
@@ -579,6 +580,7 @@
     for v, t in enumerate(lax.fori_loop(0, ZL, dots, (jnp.zeros((ROWS, LANES), F32),) * 6)):
         k.gd[v] = sum(t[8 * b:8 * b + 8] for b in range(4))
     sum_start(0, 6)
+    sum_next(0)
     parts = (k.sst, k.stg.at[0], k.stg.at[1])
 
     def out_plane(j):
@@ -617,12 +619,12 @@
         sol, res = pl.pallas_call(
             kernel,
             out_shape=(pltpu.VMEM((TL, SITE, YL), F32), pltpu.SMEM((8,), F32)),
-            in_specs=[anywhere] * 4,
+            in_specs=[anywhere] * 3 + [scalar],
             out_specs=(local, scalar),
             scratch_shapes=list(SCRATCH.values()),
-            compiler_params=pltpu.CompilerParams(collective_id=0, has_side_effects=True, vmem_limit_bytes=60000000),
+            compiler_params=pltpu.CompilerParams(collective_id=0, has_side_effects=True, vmem_limit_bytes=65000000),
             name='cg',
-        )(fat, lng, src, quark_mass.reshape(1, 1))
+        )(fat, lng, src, quark_mass)
         return jnp.transpose(sol.reshape(TL, ZL, XH, 3, 2, YL), (0, 1, 5, 2, 3, 4)), res
 
     return jax.shard_map(local_solve, mesh=mesh, in_specs=(link_spec, link_spec, field_spec, P()), out_specs=(field_spec, P()), check_vma=False)

time: 170 us -> 168 us (0.988)
  Pallas kernels: 167 us -> 165 us
    pallas_call x1, Pallas kernels: 167 us -> 165 us  [local_solve(): pl.pallas_call(kernel, out_shape=(pltpu.VMEM((TL, SITE, YL), F32), pltpu....]
where the time goes in v5:
time: 168 us
  Pallas kernels  165 us (98%)
    pallas_call x1, Pallas kernels, local_solve(): pl.pallas_call(kernel, out_shape=(pltpu.VMEM((TL, SITE, YL), F32), pltpu....  165 us

profile of v5, /device:TPU:0, one launch (start us, length us, event | category | flops | bytes accessed | tf_op | source)
XLA Modules:
  0.0 167.7 jit_solution(3089122265593126039)
XLA Ops:
  1.3 164.9 %cg.1 = (f32[6,360,48]{2,1,0:T(8,128)S(1)}, f32[8]{0:T(128)S(4)}) custom-call(f32[4,6,6,5,72,48]{5,4,3,2,1,0:T(8,128)} %bitcast.13, f32[4,6,6,5,72,48]{5,4,3,2,1,0:T(8,128)} %bitcast.14, f32[6,360,48]{2,1,0:T(8,128)} %bitcast.15, f32[1]{0:T(128)S(6)} %copy.10.mass), custom_call_target="tpu_custom_call" | custom-call | tf_op jit(solution)/shard_map/cg/pallas_call | solution.py:619
  166.2 1.0 copy.8
  167.2 0.5 copy.9

commit v6 on v5

--- a/solution.py
+++ b/solution.py
@@ -103,6 +103,10 @@
         acc[2 * i + 1] = acc[2 * i + 1] + (b * c - a * d)
 
 
+def fold(v):
+    return sum(v[first:first + 8] for first in range(0, len(v), 8))
+
+
 def rot(v, n):
     n %= LANES
     return pltpu.roll(v, n, 1) if n else v
@@ -126,6 +130,7 @@
     def remote(src_ref, dst_ref, send, recv, dev):
         return pltpu.make_async_remote_copy(src_ref=src_ref, dst_ref=dst_ref, send_sem=send, recv_sem=recv, device_id=dev, device_id_type=MESH)
 
+    everyone = [((iy + d // 8) & 3, (iz + d // 4) & 1, (it + d) & 3) for d in range(1, ROWS)]
     slab = [((iy + d // 4) & 3, iz, (it + d) & 3) for d in range(1, R0)]
 
     def plane_of(t, n2):
@@ -153,7 +158,7 @@
         for cp in stg_copies(jnp.int32(g)):
             cp.start()
     barrier = pltpu.get_barrier_semaphore()
-    for dev in slab + [at_z()]:
+    for dev in everyone:
         pl.semaphore_signal(barrier, inc=1, device_id=dev, device_id_type=MESH)
 
     lane8, row8 = (lax.broadcasted_iota(jnp.int32, (8, LANES), d) for d in (1, 0))
@@ -178,7 +183,7 @@
         return [k.f[9 * i + j, c, at(h, R0 + off), :] for c in COMPS]
 
     k.f[...] = jnp.zeros_like(k.f)
-    for ref in (k.p, k.s, k.z, k.x):
+    for ref in (k.p, k.s, k.z, k.x, k.gd):
         ref[...] = jnp.zeros_like(ref)
     k.lkt[:, :, 0:R0, :] = jnp.zeros((24, 18, R0, LANES), F32)
     k.lkt[:, :, R0 + ROWS:, :] = jnp.zeros((24, 18, 8, LANES), F32)
@@ -422,7 +427,7 @@
             gg = gg + r * r
             dd = dd + w * r
         for v, t in enumerate((gg, dd)):
-            k.gd[v] = k.gd[v] + (t[:8] + t[8:])
+            k.gd[v] = k.gd[v] + fold(t)
 
     def finish(i, t, update):
         o = 1 - i
@@ -456,30 +461,39 @@
 
         loop(0, 2, one_plane)
 
-    me = R0 + 4 * iy + it
-
     def a_copy(b, stage, first, rows, dev):
         here = k.ra.at[b, pl.ds(first, rows)]
         return remote(here, here, k.a_ss.at[b, stage], k.a_rs.at[b, stage], dev)
 
-    def sum_start(b, n):
+    def sum_start(b, n, stage, me, to):
         mine = zeros[:1]
         for v in range(n):
             total = jnp.sum(jnp.sum(k.gd[v], axis=0, keepdims=True), axis=1, keepdims=True)
             mine = jnp.where(lane[:1] == v, total, mine)
-        k.ra[b, pl.ds(iz, 1), :] = mine
-        a_copy(b, 0, iz, 1, at_z()).start()
+        k.ra[b, pl.ds(me, 1), :] = mine
+        for dev in to:
+            a_copy(b, stage, me, 1, dev).start()
 
     def sum_next(b):
         a_copy(b, 0, 0, 1, at_z()).wait()
+        me = R0 + 4 * iy + it
         k.ra[b, pl.ds(me, 1), :] = k.ra[b, 0:1, :] + k.ra[b, 1:2, :]
         for dev in slab:
             a_copy(b, 1, me, 1, dev).start()
 
-    def sum_end(b, n):
-        a_copy(b, 1, R0, len(slab), at_z()).wait()
-        tile = jnp.sum(k.ra[b, R0:], axis=0, keepdims=True)
+    def sum_end(b, n, to, first):
+        a_copy(b, 1, first, len(to), at_z()).wait()
+        tile = jnp.sum(k.ra[b, first:], axis=0, keepdims=True)
         return [jnp.broadcast_to(tile[:, v:v + 1], (8, LANES)) for v in range(n)]
+
+    def dots(q):
+        j = plane_of(jnp.where(q < 2, 0, jnp.where(q < 4, 2, 1)), lax.rem(q, 2))
+        sums = [jnp.zeros((ROWS, LANES), F32)] * 4
+        for c in COMPS:
+            w, r, s = k.f[j, c, pl.ds(R0, ROWS), :], k.r[j, c], k.s[j, c]
+            sums = [t + u * v for t, (u, v) in zip(sums, ((w, w), (r, s), (w, s), (s, s)))]
+        for v, t in enumerate(sums):
+            k.gd[2 + v] = k.gd[2 + v] + fold(t)
 
     CW, AW, AX, BETA, GAMMA, ALPHA, FIRST = range(7)
     one = jnp.ones((8, LANES), F32)
@@ -520,7 +534,7 @@
             for zi in range(ZL):
                 src_copy(zi).wait()
             loop(0, ZL, src_plane)
-            pl.semaphore_wait(barrier, R0)
+            pl.semaphore_wait(barrier, len(everyone))
 
         @pl.when(live & (i == 0) & (ph == 1) & (step > 0))
         def _():
@@ -530,8 +544,12 @@
         def _():
             @pl.when(step > 0)
             def _():
-                scalars(step, *sum_end(b, 2))
+                scalars(step, *sum_end(b, 2, slab, R0))
             k.gd[0], k.gd[1] = zero8, zero8
+
+        @pl.when((ph == 2) & jnp.logical_not(more))
+        def _():
+            loop(0, 4, dots)
 
         @pl.when(live)
         def _():
@@ -547,7 +565,7 @@
 
         @pl.when(live & (ph == 2) & (i == 1) & more)
         def _():
-            sum_start(1 - b, 2)
+            sum_start(1 - b, 2, 0, iz, [at_z()])
 
         o = jnp.where(begin, 0, 1 - i)
 
@@ -571,16 +589,8 @@
 
     loop(0, 8 + 3 * 2 * ITERS, phase)
 
-    def dots(j, carry):
-        for c in COMPS:
-            w, r, s = k.f[j, c, pl.ds(R0, ROWS), :], k.r[j, c], k.s[j, c]
-            carry = tuple(t + u * v for t, (u, v) in zip(carry, ((r, r), (w, r), (w, w), (r, s), (w, s), (s, s))))
-        return carry
-
-    for v, t in enumerate(lax.fori_loop(0, ZL, dots, (jnp.zeros((ROWS, LANES), F32),) * 6)):
-        k.gd[v] = sum(t[8 * b:8 * b + 8] for b in range(4))
-    sum_start(0, 6)
-    sum_next(0)
+    loop(4, ZL, dots)
+    sum_start(0, 6, 1, 8 * iy + 4 * iz + it, everyone)
     parts = (k.sst, k.stg.at[0], k.stg.at[1])
 
     def out_plane(j):
@@ -590,7 +600,7 @@
                     to[pl.ds(j * SITE + 6 * s + c, VALID, 12), :] = rot(frm[j, c], HALF * s)[0:VALID, 0:YL]
 
     loop(0, ZL, out_plane)
-    rr, wr, ww, rs, ws, ss = sum_end(0, 6)
+    rr, wr, ww, rs, ws, ss = sum_end(0, 6, everyone, 0)
     beta = rr / k.cf[GAMMA]
     alpha = rr / (wr - beta * rr / k.cf[ALPHA])
     last = rr - 2.0 * alpha * (wr + beta * rs) + alpha * alpha * (ww + 2.0 * beta * ws + beta * beta * ss)
@@ -613,8 +623,8 @@
     field_spec = P('t', 'zz', 'yy')
 
     def local_solve(fat_links, long_links, source, quark_mass):
-        fat, lng = (jnp.transpose(v, (0, 1, 2, 4, 5, 6, 7, 3)).reshape(4, TL, ZL, XL, QUAD, YL) for v in (fat_links, long_links))
-        src = jnp.transpose(source, (0, 1, 3, 4, 5, 2)).reshape(TL, SITE, YL)
+        fat, lng = (jnp.moveaxis(v, 3, -1).reshape(4, TL, ZL, XL, QUAD, YL) for v in (fat_links, long_links))
+        src = jnp.moveaxis(source, 2, -1).reshape(TL, SITE, YL)
         anywhere, local, scalar = (pl.BlockSpec(memory_space=space) for space in (pl.ANY, pltpu.VMEM, pltpu.SMEM))
         sol, res = pl.pallas_call(
             kernel,
@@ -625,6 +635,6 @@
             compiler_params=pltpu.CompilerParams(collective_id=0, has_side_effects=True, vmem_limit_bytes=65000000),
             name='cg',
         )(fat, lng, src, quark_mass)
-        return jnp.transpose(sol.reshape(TL, ZL, XH, 3, 2, YL), (0, 1, 5, 2, 3, 4)), res
+        return jnp.moveaxis(sol.reshape(TL, ZL, XH, 3, 2, YL), -1, 2), res
 
     return jax.shard_map(local_solve, mesh=mesh, in_specs=(link_spec, link_spec, field_spec, P()), out_specs=(field_spec, P()), check_vma=False)

time: 168 us -> 166 us (0.988)
  Pallas kernels: 165 us -> 163 us
    pallas_call x1, Pallas kernels: 165 us -> 163 us  [local_solve(): pl.pallas_call(kernel, out_shape=(pltpu.VMEM((TL, SITE, YL), F32), pltpu....]
where the time goes in v6:
time: 166 us
  Pallas kernels  163 us (98%)
    pallas_call x1, Pallas kernels, local_solve(): pl.pallas_call(kernel, out_shape=(pltpu.VMEM((TL, SITE, YL), F32), pltpu....  163 us

profile of v6, /device:TPU:0, one launch (start us, length us, event | category | flops | bytes accessed | tf_op | source)
XLA Modules:
  0.0 165.6 jit_solution(13343589348423624331)
XLA Ops:
  1.3 162.8 %cg.1 = (f32[6,360,48]{2,1,0:T(8,128)S(1)}, f32[8]{0:T(128)S(4)}) custom-call(f32[4,6,6,5,72,48]{5,4,3,2,1,0:T(8,128)} %bitcast.13, f32[4,6,6,5,72,48]{5,4,3,2,1,0:T(8,128)} %bitcast.14, f32[6,360,48]{2,1,0:T(8,128)} %bitcast.15, f32[1]{0:T(128)S(6)} %copy.10.mass), custom_call_target="tpu_custom_call" | custom-call | tf_op jit(solution)/shard_map/cg/pallas_call | solution.py:629
  164.1 1.0 copy.8
  165.1 0.5 copy.9

commit v7 on v6

--- a/solution.py
+++ b/solution.py
@@ -76,7 +76,7 @@
     f=vec(18, 6, 64), acc=plane(), cb=vec(2, 6, ROWS), xs=vec(2, 6, YL),
     r=plane(), p=plane(), s=plane(), z=plane(), x=plane(), zs=wires(), zr=wires(),
     tsf=halo_t(), trf=halo_t(), tsc=halo_t(), trc=halo_t(), ysf=halo_y(), yrf=halo_y(), ysc=halo_y(), yrc=halo_y(),
-    ra=vec(2, 32), gd=vec(6, 8), cf=vec(8, 8),
+    ra=vec(2, 32), gd=vec(7, 8), cf=vec(8, 8),
     stg_sem=sems(NSTG, 2), io_sem=sems(ZL), z_ss=sems(2), z_rs=sems(2, 6), h_ss=sems(2, 4), h_rs=sems(2, 3, 4),
     a_ss=sems(2, 2), a_rs=sems(2, 2),
 )
@@ -130,7 +130,10 @@
     def remote(src_ref, dst_ref, send, recv, dev):
         return pltpu.make_async_remote_copy(src_ref=src_ref, dst_ref=dst_ref, send_sem=send, recv_sem=recv, device_id=dev, device_id_type=MESH)
 
-    everyone = [((iy + d // 8) & 3, (iz + d // 4) & 1, (it + d) & 3) for d in range(1, ROWS)]
+    def other(d):
+        return (iy + d // 8) & 3, (iz + d // 4) & 1, (it + d) & 3
+
+    everyone = [other(d) for d in range(1, ROWS)]
     slab = [((iy + d // 4) & 3, iz, (it + d) & 3) for d in range(1, R0)]
 
     def plane_of(t, n2):
@@ -158,8 +161,7 @@
         for cp in stg_copies(jnp.int32(g)):
             cp.start()
     barrier = pltpu.get_barrier_semaphore()
-    for dev in everyone:
-        pl.semaphore_signal(barrier, inc=1, device_id=dev, device_id_type=MESH)
+    loop(1, ROWS, lambda d: pl.semaphore_signal(barrier, device_id=other(d), device_id_type=MESH))
 
     lane8, row8 = (lax.broadcasted_iota(jnp.int32, (8, LANES), d) for d in (1, 0))
     ylane8 = lane8 % HALF
@@ -278,13 +280,15 @@
         pack(lambda u, part: k.f[9 * i + m, u // 2, rows_of(u, part, R0), :], i, m)
 
     def pack_c(i, m, b, *terms):
-        for h in BLOCKS:
-            acc = [zeros] * 6
-            for n, j in terms:
-                adj(acc, lambda c: k.lko[lo(1, n, i, j), c, at(h), :], psi_of(i, j, h))
-            for c in COMPS:
-                k.cb[b, c, at(h), :] = acc[c]
+        acc = [jnp.zeros((ROWS, LANES), F32)] * 6
+        for n, j in terms:
+            adj(acc, lambda c: k.lko[lo(1, n, i, j), c], [k.f[9 * i + j, c, pl.ds(R0, ROWS), :] for c in COMPS])
+        for c in COMPS:
+            k.cb[b, c] = acc[c]
         pack(lambda u, part: k.cb[b, u // 2, rows_of(u, part), :], i, C0 + m)
+
+    def fresh(v, part):
+        return jnp.where(row8 == 0, 0.0, v) if part else v
 
     def unpack_psi(i, m):
         def store(u, part, v):
@@ -293,9 +297,17 @@
 
     def unpack_c(i, m):
         def store(u, part, v):
-            w = jnp.where(row8 == 0, 0.0, v) if part else v
-            k.acc[m, u // 2, rows_of(u, part), :] = k.acc[m, u // 2, rows_of(u, part), :] + w
+            sl = (m, u // 2, rows_of(u, part), slice(None))
+            k.acc[sl] = k.acc[sl] + fresh(v, part)
         unpack(i, C0 + m, store)
+
+    def correct(m):
+        aw = k.cf[1]
+
+        def store(u, part, v):
+            sl = (m, u // 2, rows_of(u, part, R0), slice(None))
+            k.f[sl] = k.f[sl] + aw * fresh(v, part)
+        unpack(1, C0 + m, store)
 
     def send(i, t):
         @pl.when(t == 0)
@@ -488,10 +500,10 @@
 
     def dots(q):
         j = plane_of(jnp.where(q < 2, 0, jnp.where(q < 4, 2, 1)), lax.rem(q, 2))
-        sums = [jnp.zeros((ROWS, LANES), F32)] * 4
+        sums = [jnp.zeros((ROWS, LANES), F32)] * 5
         for c in COMPS:
             w, r, s = k.f[j, c, pl.ds(R0, ROWS), :], k.r[j, c], k.s[j, c]
-            sums = [t + u * v for t, (u, v) in zip(sums, ((w, w), (r, s), (w, s), (s, s)))]
+            sums = [t + u * v for t, (u, v) in zip(sums, ((w, r), (w, w), (r, s), (w, s), (s, s)))]
         for v, t in enumerate(sums):
             k.gd[2 + v] = k.gd[2 + v] + fold(t)
 
@@ -519,9 +531,10 @@
         v = jnp.where(u > 9, u - 8, jnp.where(u > 6, 1, 0))
         n, ph = v // 3, lax.rem(v, 3)
         i = lax.rem(n, 2)
+        even, odd, starts, ends = i == 0, i == 1, ph == 0, ph == 2
         step = n // 2
         b = lax.rem(step, 2)
-        t = jnp.where(ph == 0, 0, jnp.where((ph == 1) == (i == 0), 1, 2))
+        t = jnp.where(starts, 0, jnp.where((ph == 1) == even, 1, 2))
         live = jnp.logical_not(begin)
         more = n < 2 * ITERS - 1
 
@@ -536,61 +549,66 @@
             loop(0, ZL, src_plane)
             pl.semaphore_wait(barrier, len(everyone))
 
-        @pl.when(live & (i == 0) & (ph == 1) & (step > 0))
+        @pl.when(live & even & (ph == 1) & (step > 0))
         def _():
             sum_next(b)
 
-        @pl.when(live & (i == 1) & (ph == 0))
+        @pl.when(live & odd & starts)
         def _():
             @pl.when(step > 0)
             def _():
                 scalars(step, *sum_end(b, 2, slab, R0))
             k.gd[0], k.gd[1] = zero8, zero8
 
-        @pl.when((ph == 2) & jnp.logical_not(more))
+        last = ends & jnp.logical_not(more)
+
+        @pl.when(last)
         def _():
             loop(0, 4, dots)
 
+        @pl.when(live & jnp.logical_not(last))
+        def _():
+            receive(i, t)
+
         @pl.when(live)
         def _():
-            receive(i, t)
-
-            @pl.when(i == 0)
+            @pl.when(even)
             def _():
                 finish(0, t, store_odd)
 
-            @pl.when(i == 1)
+            @pl.when(odd)
             def _():
                 finish(1, t, update_even)
 
-        @pl.when(live & (ph == 2) & (i == 1) & more)
+        @pl.when(last)
+        def _():
+            arrive(1, C0, C0 + 2)
+            loop(0, 2, lambda e: correct(2 * e))
+
+        @pl.when(live & ends & odd & more)
         def _():
             sum_start(1 - b, 2, 0, iz, [at_z()])
 
         o = jnp.where(begin, 0, 1 - i)
 
-        loop(0, jnp.where(begin, jnp.where(u < 2, u + 1, 0), jnp.where(more, 1, 0)), lambda e: send(o, jnp.where(begin, jnp.where(u == 0, 1, 2 * e), t)))
-
-        @pl.when((begin & ((u == 2) | (u == 4) | (u == 6))) | (live & more))
-        def _():
-            tell(o, jnp.where(begin, u // 2 - 1, t))
-
-        def post_one(e):
-            late = begin | (e == 2)
-            post(jnp.where(late, o, i), jnp.where(begin, u // 3 - 1, jnp.where(late, 0, e + 1)))
-
-        own = live & (ph == 0) & (n > 0)
-        next_one = jnp.where(begin, (u == 3) | (u == 7) | (u == 9), (ph == 2) & more)
-        loop(jnp.where(own, 0, 2), jnp.where(next_one, 3, 2), post_one)
-
-        @pl.when(live & (ph == 2))
+        loop(0, jnp.where(begin, jnp.where(u < 2, u + 1, 0), more.astype(jnp.int32)), lambda e: send(o, jnp.where(begin, jnp.where(u == 0, 1, 2 * e), t)))
+
+        tells = jnp.where(begin, (u == 2) | (u == 4) | (u == 6), more).astype(jnp.int32)
+        tells = jnp.where(live & (n == 0), jnp.where(starts, 1, 2 * ends.astype(jnp.int32)), tells)
+        loop(0, tells, lambda e: tell(o, jnp.where(begin, u // 2 - 1, t - e)))
+
+        @pl.when(jnp.where(begin, (u == 3) | (u == 7) | (u == 9), jnp.where(ends, more, n > 0)))
+        def _():
+            post(jnp.where(begin | ends, o, i), jnp.where(begin, u // 3 - 1, jnp.where(ends, 0, jnp.where(starts == even, 1, 2))))
+
+        @pl.when(live & ends)
         def _():
             sent(i)
 
     loop(0, 8 + 3 * 2 * ITERS, phase)
 
     loop(4, ZL, dots)
-    sum_start(0, 6, 1, 8 * iy + 4 * iz + it, everyone)
+    sum_start(0, 7, 1, 8 * iy + 4 * iz + it, everyone)
     parts = (k.sst, k.stg.at[0], k.stg.at[1])
 
     def out_plane(j):
@@ -600,7 +618,7 @@
                     to[pl.ds(j * SITE + 6 * s + c, VALID, 12), :] = rot(frm[j, c], HALF * s)[0:VALID, 0:YL]
 
     loop(0, ZL, out_plane)
-    rr, wr, ww, rs, ws, ss = sum_end(0, 6, everyone, 0)
+    rr, _, wr, ww, rs, ws, ss = sum_end(0, 7, everyone, 0)
     beta = rr / k.cf[GAMMA]
     alpha = rr / (wr - beta * rr / k.cf[ALPHA])
     last = rr - 2.0 * alpha * (wr + beta * rs) + alpha * alpha * (ww + 2.0 * beta * ws + beta * beta * ss)

time: 166 us -> 165 us (level)
  no operation moved by 1% of the time
where the time goes in v7:
time: 165 us
  Pallas kernels  162 us (98%)
    pallas_call x1, Pallas kernels, local_solve(): pl.pallas_call(kernel, out_shape=(pltpu.VMEM((TL, SITE, YL), F32), pltpu....  162 us

profile of v7, /device:TPU:0, one launch (start us, length us, event | category | flops | bytes accessed | tf_op | source)
XLA Modules:
  0.0 165.0 jit_solution(9886501373822983756)
XLA Ops:
  1.3 162.2 %cg.1 = (f32[6,360,48]{2,1,0:T(8,128)S(1)}, f32[8]{0:T(128)S(4)}) custom-call(f32[4,6,6,5,72,48]{5,4,3,2,1,0:T(8,128)} %bitcast.13, f32[4,6,6,5,72,48]{5,4,3,2,1,0:T(8,128)} %bitcast.14, f32[6,360,48]{2,1,0:T(8,128)} %bitcast.15, f32[1]{0:T(128)S(6)} %copy.10.mass), custom_call_target="tpu_custom_call" | custom-call | tf_op jit(solution)/shard_map/cg/pallas_call | solution.py:647
  163.5 1.0 copy.8
  164.5 0.5 copy.9

commit v8 on v7

--- a/solution.py
+++ b/solution.py
@@ -77,7 +77,7 @@
     r=plane(), p=plane(), s=plane(), z=plane(), x=plane(), zs=wires(), zr=wires(),
     tsf=halo_t(), trf=halo_t(), tsc=halo_t(), trc=halo_t(), ysf=halo_y(), yrf=halo_y(), ysc=halo_y(), yrc=halo_y(),
     ra=vec(2, 32), gd=vec(7, 8), cf=vec(8, 8),
-    stg_sem=sems(NSTG, 2), io_sem=sems(ZL), z_ss=sems(2), z_rs=sems(2, 6), h_ss=sems(2, 4), h_rs=sems(2, 3, 4),
+    stg_sem=sems(NSTG), io_sem=sems(1), z_ss=sems(2), z_rs=sems(2, 3), h_ss=sems(2, 2), h_rs=sems(2, 3, 2),
     a_ss=sems(2, 2), a_rs=sems(2, 2),
 )
 
@@ -150,10 +150,10 @@
 
         def to(n):
             return k.stg.at[2 * slot + n, pl.ds(0, VALID * PITCH)].reshape(TL, XL, PITCH, YL).at[:, :, pl.ds(0, QUAD)]
-        return [pltpu.make_async_copy(ref.at[di, :, zi], to(n), k.stg_sem.at[slot, n]) for n, ref in enumerate((fat, lng))]
+        return [pltpu.make_async_copy(ref.at[di, :, zi], to(n), k.stg_sem.at[slot]) for n, ref in enumerate((fat, lng))]
 
     def src_copy(zi):
-        return pltpu.make_async_copy(src.at[:, pl.ds(60 * zi, 60)], k.sst.at[pl.ds(SITE * zi, SITE)].reshape(TL, 60, YL), k.io_sem.at[zi])
+        return pltpu.make_async_copy(src.at[:, pl.ds(60 * zi, 60)], k.sst.at[pl.ds(SITE * zi, SITE)].reshape(TL, 60, YL), k.io_sem.at[0])
 
     for zi in range(ZL):
         src_copy(zi).start()
@@ -213,8 +213,9 @@
 
     def load_step(g):
         di, zi = what(g)
-        for cp in stg_copies(g):
-            cp.wait()
+        slots = pl.ds(2 * lax.rem(g, NSTG), 2)
+        used_rows = slice(TL * SITE)
+        pltpu.make_async_copy(k.stg.at[slots, used_rows], k.stg.at[slots, used_rows], k.stg_sem.at[lax.rem(g, NSTG)]).wait()
 
         @pl.when(di == 0)
         def _():
@@ -229,21 +230,24 @@
             for cp in stg_copies(g + NSTG):
                 cp.start()
 
-    def z_copy(i, m):
-        return remote(k.zs.at[i, m, used], k.zr.at[i, m, used], k.z_ss.at[i], k.z_rs.at[i, m], at_z())
-
-    def h_copies(i, t, whole=False):
+    def z_copy(i, m, t):
+        return remote(k.zs.at[i, m, used], k.zr.at[i, m, used], k.z_ss.at[i], k.z_rs.at[i, t], at_z())
+
+    def h_copies(i, t):
         pairs = ((k.tsf, k.trf, at_t(3)), (k.tsc, k.trc, at_t(1)), (k.ysf, k.yrf, at_y(3)), (k.ysc, k.yrc, at_y(1)))
-        some = pl.ds(0, ZL) if whole else pl.ds(2 * t, 2)
-        return [remote(a.at[i, some], b.at[i, some], k.h_ss.at[i, n], k.h_rs.at[i, t, n], dev) for n, (a, b, dev) in enumerate(pairs)]
+        two = pl.ds(2 * t, 2)
+        return [remote(a.at[i, two], b.at[i, two], k.h_ss.at[i, n // 2], k.h_rs.at[i, t, n // 2], dev) for n, (a, b, dev) in enumerate(pairs)]
+
+    def h_waits(i, t, *some):
+        return [remote(a.at[some], b.at[some], k.h_ss.at[i, n], k.h_rs.at[i, t, n], at_t(1)) for n, (a, b) in enumerate(((k.tsf, k.trf), (k.ysf, k.yrf)))]
 
     def sent(i):
         remote(k.zs.at[i, :, used], k.zr.at[i, :, used], k.z_ss.at[i], k.z_rs.at[i, 0], at_z()).wait_send()
-        for cp in h_copies(i, 0, True):
+        for cp in h_waits(i, 0, slice(None)):
             cp.wait_send()
 
     gap = ylane8 >= YL
-    used = pl.ds(0, 135)
+    used = slice(135)
 
     def rows_of(u, part, off=0):
         return pl.ds(off + 15 * (u % 2) + part, 8)
@@ -268,13 +272,11 @@
                     guest = jnp.where(ylane8 // R0 == q, rot(h, R0 * q - YL), guest)
                 store(9 + u, part, guest)
 
-    def start(i, *ms):
-        for m in ms:
-            z_copy(i, m).start()
-
-    def arrive(i, *ms):
-        for m in ms:
-            z_copy(i, m).wait_recv()
+    def start(i, m, t):
+        z_copy(i, m, t).start()
+
+    def arrive(i, t):
+        z_copy(i, slice(2), t).wait_recv()
 
     def pack_psi(i, m):
         pack(lambda u, part: k.f[9 * i + m, u // 2, rows_of(u, part, R0), :], i, m)
@@ -313,37 +315,39 @@
         @pl.when(t == 0)
         def _():
             pack_psi(i, 1)
+            start(i, 1, 0)
             pack_c(i, 1, 0, (1, 4))
-            start(i, 1, C0 + 1)
+            start(i, C0 + 1, 0)
 
         @pl.when(t == 1)
         def _():
-            pack_psi(i, 0)
-            pack_psi(i, 2)
-            start(i, 0, 2)
+            for m in (0, 2):
+                pack_psi(i, m)
+                start(i, m, 2)
 
         @pl.when(t == 2)
         def _():
+            pack_c(i, 2, 1, (1, 5))
+            start(i, C0 + 2, 1)
             pack_c(i, 0, 0, (0, 5), (1, 3))
-            pack_c(i, 2, 1, (1, 5))
-            start(i, C0, C0 + 2)
+            start(i, C0, 1)
 
     def receive(i, t):
         @pl.when(t == 0)
         def _():
-            arrive(i, 1, C0 + 1)
+            arrive(i, t)
             unpack_psi(i, 1)
             unpack_c(i, 1)
 
         @pl.when(t == 1)
         def _():
-            arrive(i, C0, C0 + 2)
+            arrive(i, t)
             unpack_c(i, 0)
             unpack_c(i, 2)
 
         @pl.when(t == 2)
         def _():
-            arrive(i, 0, 2)
+            arrive(i, t)
             unpack_psi(i, 0)
             unpack_psi(i, 2)
 
@@ -354,17 +358,19 @@
             fwd, bwd = zeros, zeros
             for h in BLOCKS:
                 psi = psi_of(i, j, h)
-                back = [zeros] * 6
+                chis = []
                 for n, off in STEPS:
-                    chi = [zeros] * 6
-                    adj(chi, lambda c: k.lko[lo(2, n, i, j), c, at(h), :], psi)
-                    back = [back[c] + rot(chi[c], off) for c in COMPS]
+                    chis.append([zeros] * 6)
+                    adj(chis[n], lambda c: k.lko[lo(2, n, i, j), c, at(h), :], psi)
                 for c in COMPS:
-                    k.acc[j, c, at(h), :] = back[c]
+                    def back(by):
+                        near, far = (rot(chis[n][c], off + by) for n, off in STEPS)
+                        return near + far
+                    k.acc[j, c, at(h), :] = back(0)
                     to = 4 * c + 24 * (h // BLK)
                     here = ylane // 4 == to // 4
                     fwd = jnp.where(here, rot(psi[c], to), fwd)
-                    bwd = jnp.where(here, rot(back[c], to - YL), bwd)
+                    bwd = jnp.where(here, back(to - YL), bwd)
             k.ysf[i, slot] = fwd
             k.ysc[i, slot] = bwd
             for h in range(2):
@@ -443,7 +449,7 @@
 
     def finish(i, t, update):
         o = 1 - i
-        for cp in h_copies(i, t):
+        for cp in h_waits(i, t, i, slice(4)):
             cp.wait_recv()
 
         def one_plane(n2):
@@ -544,8 +550,8 @@
 
         @pl.when(u == 0)
         def _():
-            for zi in range(ZL):
-                src_copy(zi).wait()
+            all_rows = k.sst.at[:ZL * SITE]
+            pltpu.make_async_copy(all_rows, all_rows, k.io_sem.at[0]).wait()
             loop(0, ZL, src_plane)
             pl.semaphore_wait(barrier, len(everyone))
 
@@ -582,7 +588,7 @@
 
         @pl.when(last)
         def _():
-            arrive(1, C0, C0 + 2)
+            arrive(i, t)
             loop(0, 2, lambda e: correct(2 * e))
 
         @pl.when(live & ends & odd & more)

time: 165 us -> 165 us (level)
  no operation moved by 1% of the time
where the time goes in v8:
time: 165 us
  Pallas kernels  162 us (98%)
    pallas_call x1, Pallas kernels, local_solve(): pl.pallas_call(kernel, out_shape=(pltpu.VMEM((TL, SITE, YL), F32), pltpu....  162 us

profile of v8, /device:TPU:0, one launch (start us, length us, event | category | flops | bytes accessed | tf_op | source)
XLA Modules:
  0.0 164.6 jit_solution(13854624955164160184)
XLA Ops:
  1.3 161.8 %cg.1 = (f32[6,360,48]{2,1,0:T(8,128)S(1)}, f32[8]{0:T(128)S(4)}) custom-call(f32[4,6,6,5,72,48]{5,4,3,2,1,0:T(8,128)} %bitcast.13, f32[4,6,6,5,72,48]{5,4,3,2,1,0:T(8,128)} %bitcast.14, f32[6,360,48]{2,1,0:T(8,128)} %bitcast.15, f32[1]{0:T(128)S(6)} %copy.10.mass), custom_call_target="tpu_custom_call" | custom-call | tf_op jit(solution)/shard_map/cg/pallas_call | solution.py:653
  163.1 1.0 copy.8
  164.1 0.5 copy.9

commit v9 on v8

--- a/solution.py
+++ b/solution.py
@@ -356,21 +356,18 @@
             j = plane_of(t, n2)
             slot = 2 * t + n2
             fwd, bwd = zeros, zeros
-            for h in BLOCKS:
-                psi = psi_of(i, j, h)
-                chis = []
-                for n, off in STEPS:
-                    chis.append([zeros] * 6)
-                    adj(chis[n], lambda c: k.lko[lo(2, n, i, j), c, at(h), :], psi)
-                for c in COMPS:
-                    def back(by):
-                        near, far = (rot(chis[n][c], off + by) for n, off in STEPS)
-                        return near + far
-                    k.acc[j, c, at(h), :] = back(0)
+            psi = [k.f[9 * i + j, c, pl.ds(R0, ROWS), :] for c in COMPS]
+            chis = []
+            for n, _ in STEPS:
+                chis.append([jnp.zeros((ROWS, LANES), F32)] * 6)
+                adj(chis[n], lambda c: k.lko[lo(2, n, i, j), c], psi)
+            for c in COMPS:
+                k.acc[j, c] = sum(rot(chis[n][c], off) for n, off in STEPS)
+                for h in BLOCKS:
                     to = 4 * c + 24 * (h // BLK)
                     here = ylane // 4 == to // 4
-                    fwd = jnp.where(here, rot(psi[c], to), fwd)
-                    bwd = jnp.where(here, back(to - YL), bwd)
+                    fwd = jnp.where(here, rot(psi[c][h:h + BLK], to), fwd)
+                    bwd = jnp.where(here, sum(rot(chis[n][c][h:h + BLK], to - YL + off) for n, off in STEPS), bwd)
             k.ysf[i, slot] = fwd
             k.ysc[i, slot] = bwd
             for h in range(2):
@@ -382,7 +379,8 @@
                     k.tsc[i, slot, c, pl.ds(8 * h, 8), :] = acc[c]
                     k.tsf[i, slot, c, pl.ds(8 * h, 8), :] = k.f[9 * i + j, c, pl.ds(R0 + 8 * h, 8), :]
 
-        loop(0, 2, one_plane)
+        for n2 in range(2):
+            one_plane(n2)
         for cp in h_copies(i, t):
             cp.start()
 

time: 165 us -> 165 us (level)
  no operation moved by 1% of the time
where the time goes in v9:
time: 165 us
  Pallas kernels  162 us (98%)
    pallas_call x1, Pallas kernels, local_solve(): pl.pallas_call(kernel, out_shape=(pltpu.VMEM((TL, SITE, YL), F32), pltpu....  162 us

profile of v9, /device:TPU:0, one launch (start us, length us, event | category | flops | bytes accessed | tf_op | source)
XLA Modules:
  0.0 164.5 jit_solution(4194820520621570901)
XLA Ops:
  1.3 161.7 %cg.1 = (f32[6,360,48]{2,1,0:T(8,128)S(1)}, f32[8]{0:T(128)S(4)}) custom-call(f32[4,6,6,5,72,48]{5,4,3,2,1,0:T(8,128)} %bitcast.13, f32[4,6,6,5,72,48]{5,4,3,2,1,0:T(8,128)} %bitcast.14, f32[6,360,48]{2,1,0:T(8,128)} %bitcast.15, f32[1]{0:T(128)S(6)} %copy.10.mass), custom_call_target="tpu_custom_call" | custom-call | tf_op jit(solution)/shard_map/cg/pallas_call | solution.py:651
  163.0 1.0 copy.8
  164.0 0.5 copy.9
